TPU v7x, 32 devices: a whole 2x2x4 slice. The times are simulated.
32 devices in a mesh: node: 8 (over z, x), local: 4 (over y, core).
Axes of the slice: x: 2, y: 2, z: 4, core: 2. Of those that a mesh axis runs over, the one named last changes fastest.
Arguments:
- tokens: bfloat16 [128, 3584], P(('node', 'local')), may hold values from -6 to 6
- expert_ids: int32 [128, 6], P(('node', 'local')), may hold values from 0 to 15, as said below
- gate_codes: int32 [128, 6], P(('node', 'local')), may hold values from 1 to 1023
- gate_proj: bfloat16 [3584, 16384], P(None, ('node', 'local')), may hold values from -0.09375 to 0.09375
- up_proj: bfloat16 [3584, 16384], P(None, ('node', 'local')), may hold values from -0.09375 to 0.09375
- down_proj: bfloat16 [16384, 3584], P('node', 'local'), may hold values from -0.1875 to 0.1875
Outputs:
- routed: bfloat16 [128, 3584], P(('node', 'local'))
Inputs may be any that keep to these rules, and one draw needn't show every extreme that they name: `expert_ids`: each token names 6 different experts, lying in exactly 4 node groups with at least one named expert in each. The tokens of one device name each node group at most 2 times in all and some node group exactly 2 times; where 8 divides 4 * 4, they name every node group exactly 2 times. For every local index, the tokens of all devices with that local index together name each node group exactly 4 * 4 times.
All inputs are finite; a program needn't handle non-finite values.
Results may differ from a plain program's by a relative error of at most 0.02.
Values may be sent and summed in bfloat16 or wider, within the bound.
No kernel may reach another device: no remote copies, remote signals or barrier semaphores. Data moves between devices by JAX's collectives and lax.ppermute only.
A program may use at most 64 MiB of HBM per device.

v0:
```python
import jax
import jax.numpy as jnp
from jax import lax
from jax.sharding import PartitionSpec as P

FF_E = 1024
EXP_NODE = 2
NL = 4


ROUTE_SCALE = 2.5


def shortened(array):

    def short(part):
        return part.astype(jnp.bfloat16) if part.dtype == jnp.float32 else part

    return jax.tree.map(short, array)


def on_device(tokens, expert_ids, gate_codes, gate_proj, up_proj, down_proj):
    node_count = lax.axis_size("node")
    own_rows, model_width = tokens.shape
    slot_cap = -(-(own_rows * NL) // node_count)
    kept_rows = own_rows * NL
    node_of = expert_ids // EXP_NODE
    expert_side = expert_ids % EXP_NODE
    node_hit = node_of[:, :, None] == jnp.arange(node_count, dtype=jnp.int32)[None, None, :]
    code_pair = jnp.stack(
        [
            jnp.sum(
                jnp.where(
                    node_hit & (expert_side == side_index)[:, :, None], gate_codes[:, :, None], 0
                ),
                axis=1,
            )
            for side_index in range(EXP_NODE)
        ],
        axis=2,
    )
    node_used = jnp.any(node_hit, axis=1).astype(jnp.int32)
    code_total = jnp.sum(gate_codes, axis=1)
    token_info = jnp.concatenate([code_pair, (code_total[:, None] * node_used)[:, :, None]], axis=2)
    slot_rank = jnp.cumsum(node_used, axis=0) - node_used
    slot_hot = node_used[:, :, None] * (
        slot_rank[:, :, None] == jnp.arange(slot_cap, dtype=jnp.int32)[None, None, :]
    ).astype(jnp.int32)
    placing = slot_hot.astype(jnp.bfloat16)
    send_rows = jnp.einsum(
        "tnc,td->ncd", placing, tokens, preferred_element_type=jnp.float32
    ).astype(jnp.bfloat16)
    send_info = jnp.sum(slot_hot[:, :, :, None] * token_info[:, :, None, :], axis=0)
    arrived, arrived_info = (
        lax.all_to_all(send_rows, "node", split_axis=0, concat_axis=0, tiled=True),
        lax.all_to_all(send_info, "node", split_axis=0, concat_axis=0, tiled=True),
    )
    flat_rows = arrived.reshape(node_count * slot_cap, model_width)
    flat_info = arrived_info.reshape(node_count * slot_cap, EXP_NODE + 1)
    slot_live = (flat_info[:, EXP_NODE] > 0).astype(jnp.int32)
    position = jnp.cumsum(slot_live) - slot_live
    target_row = jnp.where(slot_live > 0, position, kept_rows)
    source_row = (
        jnp.zeros((kept_rows,), jnp.int32)
        .at[target_row]
        .set(jnp.arange(node_count * slot_cap, dtype=jnp.int32), mode="drop")
    )
    compact_rows = jnp.take(flat_rows, source_row, axis=0)
    compact_info = jnp.take(flat_info, source_row, axis=0)
    per_lane = gate_proj.shape[1]
    node_tokens, node_info = (
        lax.all_gather(compact_rows, "local", axis=0, tiled=True),
        lax.all_gather(shortened(compact_info), "local", axis=0, tiled=True).astype(
            compact_info.dtype
        ),
    )
    pre_gate = jnp.dot(node_tokens, gate_proj, preferred_element_type=jnp.float32)
    pre_up = jnp.dot(node_tokens, up_proj, preferred_element_type=jnp.float32)
    mine_expert = lax.axis_index("local") * per_lane // FF_E
    code_mine = jnp.sum(
        jnp.where(
            jnp.arange(EXP_NODE, dtype=jnp.int32)[None, :] == mine_expert,
            node_info[:, :EXP_NODE],
            0,
        ),
        axis=1,
    )
    gate_weight = (
        ROUTE_SCALE * code_mine.astype(jnp.float32) / node_info[:, EXP_NODE].astype(jnp.float32)
    )
    hidden = (gate_weight[:, None] * jax.nn.silu(pre_gate) * pre_up).astype(jnp.bfloat16)
    contrib = jnp.dot(
        lax.all_gather(hidden, "local", axis=1, tiled=True),
        down_proj,
        preferred_element_type=jnp.float32,
    ).astype(jnp.bfloat16)
    own_result = lax.all_to_all(contrib, "local", split_axis=0, concat_axis=1, tiled=True)
    back_index = jnp.minimum(position, kept_rows - 1)
    slot_back = jnp.where(
        slot_live[:, None] > 0,
        jnp.take(own_result, back_index, axis=0),
        jnp.zeros((), jnp.bfloat16),
    )
    returned = lax.all_to_all(
        slot_back.reshape(node_count, slot_cap, model_width),
        "node",
        split_axis=0,
        concat_axis=0,
        tiled=True,
    )
    return jnp.einsum("tnc,ncd->td", placing, returned, preferred_element_type=jnp.float32).astype(
        jnp.bfloat16
    )


def solution(mesh):
    return jax.shard_map(
        on_device,
        mesh=mesh,
        in_specs=(
            P(("node", "local"), None),
            P(("node", "local"), None),
            P(("node", "local"), None),
            P(None, ("node", "local")),
            P(None, ("node", "local")),
            P("node", "local"),
        ),
        out_specs=P(("node", "local"), None),
        check_vma=False,
    )
```

profile of v0, /device:TPU:0, one launch (start us, length us, event | category | flops | bytes accessed | tf_op | source)
XLA Modules:
  0.0 69.7 jit_solution(9421416398679059585)
XLA Ops:
  0.0 0.0 copy-start
  0.0 0.7 add_select_fusion.1
  0.7 0.7 broadcast_compare_fusion.3
  1.4 0.1 copy.32
  1.5 0.1 fusion.6
  1.6 0.8 %copy.34 = s32[4,6]{0,1:T(8,128)S(1)} copy(s32[4,6]{1,0:T(4,128)} %param.10) | data formatting | bytes 192 | tf_op args[2]
  2.4 0.8 %reduce_sum.47 = s32[4]{0:T(128)S(1)} reduce(s32[4,6]{1,0:T(4,128)} %param.10, s32[]{:T(128)} %constant.81.clone.1), dimensions={1}, to_apply=%region_4.5 | reduce | flops 20 | bytes 116 | tf_op jit(solution)/shard_map/reduce_sum | solution.py:43
  3.2 0.1 copy.33
  3.3 0.1 copy.35
  3.4 0.1 bitcast_select_fusion
  3.5 0.1 select_reduce_fusion.1
  3.6 0.7 copy.36
  4.3 7.3 %all-to-all-start = ((s32[8,2,3]{2,1,0:T(2,128)}), s32[8,2,3]{2,1,0:T(2,128)S(1)}, u32[]{:S(2)}, u32[]{:S(2)}) async-start(s32[8,2,3]{2,1,0:T(2,128)} %copy.36), calls=%async_computation | async-start | bytes 16384 | tf_op jit(solution)/shard_map/all_to_all | solution.py:56
  11.6 0.0 copy-done
  11.6 0.2 convolution_convert_fusion
  11.9 0.7 %copy.42 = bf16[8,2,3584]{2,1,0:T(2,128)(2,1)} copy(bf16[8,2,3584]{2,0,1:T(8,128)(2,1)S(1)} %convolution_convert_fusion) | data formatting | bytes 229376 | tf_op jit(solution)/shard_map/convert_element_type | solution.py:52
  12.6 5.5 %all-to-all-done = s32[8,2,3]{2,1,0:T(2,128)S(1)} async-done(((s32[8,2,3]{2,1,0:T(2,128)}), s32[8,2,3]{2,1,0:T(2,128)S(1)}, u32[]{:S(2)}, u32[]{:S(2)}) %all-to-all-start) | async-done | bytes 224 | tf_op jit(solution)/shard_map/all_to_all | solution.py:56
  18.1 3.4 %all-to-all-start.1 = ((bf16[8,2,3584]{2,1,0:T(2,128)(2,1)}), bf16[8,2,3584]{2,1,0:T(2,128)(2,1)S(1)}, u32[]{:S(2)}, u32[]{:S(2)}) async-start(bf16[8,2,3584]{2,1,0:T(2,128)(2,1)} %copy.42), calls=%async_computation.1 | async-start | bytes 229376 | tf_op jit(solution)/shard_map/all_to_all | solution.py:55
  21.5 0.2 fusion.16
  21.7 0.2 minimum_reduce_fusion
  21.9 0.6 scatter_custom_fusion
  22.6 0.6 gather_fusion
  23.1 0.1 broadcast_select_fusion.1
  23.2 0.1 copy.40
  23.3 5.2 %all-gather = s32[4,16,3]{1,2,0:T(4,128)S(1)} all-gather(s32[1,16,3]{1,2,0:T(4,128)S(1)} %bitcast.36), channel_id=1, replica_groups=mesh['node'=8,'local'=4] {'local'}, dimensions={0}, use_global_device_ids=true | all-gather | bytes 960 | tf_op jit(solution)/shard_map/all_gather | solution.py:73
  28.5 0.1 reshape.142
  28.6 0.1 select_reduce_fusion.2
  28.7 0.0 all-to-all-done.1
  28.8 0.6 gather_fusion.1
  29.4 0.0 copy-start.1
  29.4 0.1 broadcast_select_fusion
  29.5 7.1 %all_gather.10 = bf16[64,3584]{1,0:T(8,128)(2,1)S(1)} all-gather(bf16[16,3584]{1,0:T(8,128)(2,1)S(1)} %broadcast_select_fusion), channel_id=1, replica_groups=mesh['node'=8,'local'=4] {'local'}, dimensions={0}, use_global_device_ids=true | all-gather | bytes 573440 | tf_op jit(solution)/shard_map/all_gather | solution.py:72
  36.5 0.0 copy-start.2
  36.5 2.9 %fusion.19 = f32[64,512]{1,0:T(8,128)S(1)} fusion(bf16[64,3584]{1,0:T(8,128)(2,1)S(1)} %all_gather.10, bf16[3584,512]{1,0:T(8,128)(2,1)} %param.11), kind=kOutput, calls=%fused_computation.58 | convolution fusion | flops 234881024 | bytes 4259840 | tf_op jit(solution)/shard_map/dot_general | solution.py:77
  39.5 0.0 copy-done.1
  39.5 0.7 %fusion.1 = bf16[64,512]{1,0:T(8,128)(2,1)S(1)} fusion(bf16[64,3584]{1,0:T(8,128)(2,1)S(1)} %all_gather.10, bf16[3584,512]{1,0:T(8,128)(2,1)S(1)} %copy-done.1, f32[64,512]{1,0:T(8,128)S(1)} %fusion.19, f32[64]{0:T(128)S(1)} %fusion.13), kind=kOutput, calls=%fused_computation.9 | convolution fusion | flops 235110400 | bytes 4325632 | tf_op jit(solution)/shard_map/dot_general | solution.py:78
  40.2 5.9 %all_gather.11 = bf16[64,2048]{1,0:T(8,128)(2,1)S(1)} all-gather(bf16[64,512]{1,0:T(8,128)(2,1)S(1)} %fusion.1), channel_id=1, replica_groups=mesh['node'=8,'local'=4] {'local'}, dimensions={1}, use_global_device_ids=true | all-gather | bytes 327680 | tf_op jit(solution)/shard_map/all_gather | solution.py:93
  46.1 0.0 copy-done.2
  46.1 1.4 %convolution_convert_fusion.1 = bf16[64,896]{1,0:T(8,128)(2,1)} fusion(bf16[64,2048]{1,0:T(8,128)(2,1)S(1)} %all_gather.11, bf16[2048,896]{1,0:T(8,128)(2,1)S(1)} %copy-done.2), kind=kOutput, calls=%fused_computation.7 | convolution fusion | flops 234938368 | bytes 4046848 | tf_op jit(solution)/shard_map/dot_general | solution.py:92
  47.4 3.3 %all-to-all-start.2 = ((bf16[4,16,896]{2,1,0:T(8,128)(2,1)}), bf16[4,16,896]{2,1,0:T(8,128)(2,1)S(1)}, u32[]{:S(2)}, u32[]{:S(2)}) async-start(bf16[4,16,896]{2,1,0:T(8,128)(2,1)} %bitcast.8), calls=%async_computation.2 | async-start | bytes 229376 | tf_op jit(solution)/shard_map/all_to_all | solution.py:97
  50.8 4.4 %all-to-all-done.2 = bf16[4,16,896]{2,1,0:T(8,128)(2,1)S(1)} async-done(((bf16[4,16,896]{2,1,0:T(8,128)(2,1)}), bf16[4,16,896]{2,1,0:T(8,128)(2,1)S(1)}, u32[]{:S(2)}, u32[]{:S(2)}) %all-to-all-start.2) | async-done | bytes 114720 | tf_op jit(solution)/shard_map/all_to_all | solution.py:97
  55.2 0.6 gather_fusion.2
  55.8 0.1 select_select_fusion
  55.9 13.0 %all_to_all.34 = bf16[8,2,3584]{2,1,0:T(2,128)(2,1)S(1)} all-to-all(bf16[8,2,3584]{2,1,0:T(2,128)(2,1)S(1)} %reshape.105), channel_id=1, replica_groups=mesh['node'=8,'local'=4] {'node'}, dimensions={0} | all-to-all | bytes 229376 | tf_op jit(solution)/shard_map/all_to_all | solution.py:104
  68.9 0.8 %fusion = bf16[4,3584]{1,0:T(4,128)(2,1)} fusion(bf16[8,2,3584]{2,1,0:T(2,128)(2,1)S(1)} %all_to_all.34, s32[4,8]{1,0:T(4,128)S(1)} %convert_element_type.52, s32[4,8]{1,0:T(4,128)S(1)} %convert_subtract_fusion), kind=kOutput, calls=%fused_computation.6 | convolution fusion | flops 473280 | bytes 143616 | tf_op jit(solution)/shard_map/tnc,ncd->td/dot_general | solution.py:111
  (20 shorter events, 0.3 us)
Async XLA Ops:
  0.0 11.6 %copy-start = (bf16[4,3584]{1,0:T(4,128)(2,1)S(1)}, bf16[4,3584]{1,0:T(4,128)(2,1)}, u32[]{:S(2)}) copy-start(bf16[4,3584]{1,0:T(4,128)(2,1)} %param.8) | copy-start | bytes 86020
  4.3 13.8 %all-to-all-start = ((s32[8,2,3]{2,1,0:T(2,128)}), s32[8,2,3]{2,1,0:T(2,128)S(1)}, u32[]{:S(2)}, u32[]{:S(2)}) async-start(s32[8,2,3]{2,1,0:T(2,128)} %copy.36), calls=%async_computation | async-start | bytes 16384 | tf_op jit(solution)/shard_map/all_to_all | solution.py:56
  18.1 10.6 %all-to-all-start.1 = ((bf16[8,2,3584]{2,1,0:T(2,128)(2,1)}), bf16[8,2,3584]{2,1,0:T(2,128)(2,1)S(1)}, u32[]{:S(2)}, u32[]{:S(2)}) async-start(bf16[8,2,3584]{2,1,0:T(2,128)(2,1)} %copy.42), calls=%async_computation.1 | async-start | bytes 229376 | tf_op jit(solution)/shard_map/all_to_all | solution.py:55
  29.4 10.1 %copy-start.1 = (bf16[3584,512]{1,0:T(8,128)(2,1)S(1)}, bf16[3584,512]{1,0:T(8,128)(2,1)}, u32[]{:S(2)}) copy-start(bf16[3584,512]{1,0:T(8,128)(2,1)} %param.12) | copy-start | bytes 11010052
  36.5 9.6 %copy-start.2 = (bf16[2048,896]{1,0:T(8,128)(2,1)S(1)}, bf16[2048,896]{1,0:T(8,128)(2,1)}, u32[]{:S(2)}) copy-start(bf16[2048,896]{1,0:T(8,128)(2,1)} %param.13) | copy-start | bytes 11010052
  47.4 7.7 %all-to-all-start.2 = ((bf16[4,16,896]{2,1,0:T(8,128)(2,1)}), bf16[4,16,896]{2,1,0:T(8,128)(2,1)S(1)}, u32[]{:S(2)}, u32[]{:S(2)}) async-start(bf16[4,16,896]{2,1,0:T(8,128)(2,1)} %bitcast.8), calls=%async_computation.2 | async-start | bytes 229376 | tf_op jit(solution)/shard_map/all_to_all | solution.py:97
where the time goes:
time: 70.2 us; the launch traced here: 69.7 us
  blocking collectives  31.1 us (44%)
  starting transfers between devices  14 us (20%)
  waiting for transfers between devices  9.91 us (14%)
  matrix products  6.06 us (9%)
  local copies, waits for them, and re-layouts  5.2 us (7%)
  other arithmetic  3.32 us (5%)
    all_to_all x1, blocking collectives, on_device(): lax.all_to_all(slot_back.reshape(node_count, slot_cap, model_width), 'nod...  13 us
    all_to_all x1, starting transfers between devices, on_device(): lax.all_to_all(send_info, 'node', split_axis=0, concat_axis=0, tiled=True)  7.28 us
    all_gather x1, blocking collectives, on_device(): lax.all_gather(compact_rows, 'local', axis=0, tiled=True)  7.05 us
    all_gather x1, blocking collectives, on_device(): lax.all_gather(hidden, 'local', axis=1, tiled=True)  5.86 us
    all_to_all x1, waiting for transfers between devices, on_device(): lax.all_to_all(send_info, 'node', split_axis=0, concat_axis=0, tiled=True)  5.53 us
    all_gather x1, blocking collectives, on_device(): lax.all_gather(shortened(compact_info), 'local', axis=0, tiled=True)  5.18 us
    all_to_all x1, waiting for transfers between devices, on_device(): lax.all_to_all(contrib, 'local', split_axis=0, concat_axis=1, tiled=True)  4.38 us
    all_to_all x1, starting transfers between devices, on_device(): lax.all_to_all(send_rows, 'node', split_axis=0, concat_axis=0, tiled=True)  3.37 us
  transfers between devices with their start and end apart: 3, of which 2 were waited for; matrix products, arithmetic and copies ran while one was open for 4% of the time, Pallas kernels for 0%

commit v1 on v0

v1 whole, which is shorter than its diff:
```python
import functools

import jax
import jax.numpy as jnp
from jax import lax
from jax.experimental import pallas as pl
from jax.experimental.pallas import tpu as pltpu
from jax.sharding import PartitionSpec as P

FF_E = 1024
EXP_NODE = 2
NL = 4
ROUTE_SCALE = 2.5
LANES = 128
EVERY = ("node", "local")


def slot_mask(ids, group, slot):
    rows = ids.shape[0]
    node_of = ids // EXP_NODE
    used = jnp.zeros(group.shape, jnp.bool_)
    for k in range(ids.shape[1]):
        used = used | (node_of[:, k : k + 1] == group)
    used = used.astype(jnp.int32)
    ranks, so_far = [], jnp.zeros((1, group.shape[1]), jnp.int32)
    for t in range(rows):
        ranks.append(so_far)
        so_far = so_far + used[t : t + 1]
    rank = jnp.concatenate(ranks, axis=0)
    return jnp.where((used > 0) & (rank == slot), 1.0, 0.0)


def dispatch_kernel(nodes, lanes_local, slots, tok_ref, ids_ref, codes_ref, out_ref):
    ids = ids_ref[...]
    rows, top = ids.shape
    width = tok_ref.shape[1]
    half = width // 2
    codes = codes_ref[...].astype(jnp.float32)
    weight = ROUTE_SCALE * codes / jnp.sum(codes, axis=1, keepdims=True)
    high = weight.astype(jnp.bfloat16).astype(jnp.float32)
    middle = (weight - high).astype(jnp.bfloat16).astype(jnp.float32)
    low = weight - high - middle
    lane = lax.broadcasted_iota(jnp.int32, (rows, LANES), 1)
    score = jnp.zeros((rows, LANES), jnp.float32)
    for part, values in enumerate((ids.astype(jnp.float32), high, middle, low)):
        for k in range(top):
            score = jnp.where(lane == part * top + k, values[:, k : k + 1], score)
    count = nodes * slots
    spot = lax.broadcasted_iota(jnp.int32, (rows, count), 1)
    mask = slot_mask(ids, spot // slots, spot % slots).astype(jnp.bfloat16)
    contract = (((0,), (0,)), ((), ()))
    placed = lax.dot_general(mask, tok_ref[...], contract, preferred_element_type=jnp.float32).astype(jnp.bfloat16)
    scored = lax.dot_general(
        mask, score.astype(jnp.bfloat16), contract, preferred_element_type=jnp.float32
    ).astype(jnp.bfloat16)
    for n in range(nodes):
        own = slice(n * slots, (n + 1) * slots)
        for l in range(lanes_local):
            side = l % 2
            out_ref[n * lanes_local + l, :, :half] = placed[own, side * half : (side + 1) * half]
            out_ref[n * lanes_local + l, :, half:] = scored[own]


def combine_kernel(nodes, lanes_local, slots, ids_ref, back_ref, out_ref):
    ids = ids_ref[...]
    rows = ids.shape[0]
    piece = back_ref.shape[1]
    count = nodes * lanes_local * slots
    spot = lax.broadcasted_iota(jnp.int32, (rows, count), 1)
    mask = slot_mask(ids, spot // (lanes_local * slots), spot % slots)
    owner = (spot // slots) % lanes_local
    pick = jnp.concatenate([jnp.where(owner == l, mask, 0.0) for l in range(lanes_local)], axis=0)
    summed = jnp.dot(pick.astype(jnp.bfloat16), back_ref[...], preferred_element_type=jnp.float32)
    for l in range(lanes_local):
        out_ref[:, l * piece : (l + 1) * piece] = summed[l * rows : (l + 1) * rows].astype(jnp.bfloat16)


def on_device(tokens, expert_ids, gate_codes, gate_proj, up_proj, down_proj):
    nodes, locals_ = lax.axis_size("node"), lax.axis_size("local")
    own_rows, width = tokens.shape
    slots = -(-(own_rows * NL) // nodes)
    devices = nodes * locals_
    half = width // 2
    send = pl.pallas_call(
        functools.partial(dispatch_kernel, nodes, locals_, slots),
        out_shape=jax.ShapeDtypeStruct((devices, slots, half + LANES), jnp.bfloat16),
        name="dispatch",
    )(tokens, expert_ids, gate_codes)
    arrived = lax.all_to_all(send, EVERY, split_axis=0, concat_axis=0, tiled=True)
    arrived = arrived.reshape(devices * slots, half + LANES)
    mine, score = arrived[:, :half], arrived[:, half:].astype(jnp.float32)
    other = lax.ppermute(mine, "local", [(i, i ^ 1) for i in range(locals_)])
    local = lax.axis_index("local")
    chosen = jnp.where(
        local % 2 == 0,
        jnp.concatenate([mine, other], axis=1),
        jnp.concatenate([other, mine], axis=1),
    )
    per_lane = gate_proj.shape[1]
    expert = lax.axis_index("node") * EXP_NODE + local * per_lane // FF_E
    top = expert_ids.shape[1]
    named = score[:, :top] == expert.astype(jnp.float32)
    weight = score[:, top : 2 * top] + score[:, 2 * top : 3 * top] + score[:, 3 * top : 4 * top]
    gate = jnp.sum(jnp.where(named, weight, 0.0), axis=1, keepdims=True)
    pre_gate = jnp.dot(chosen, gate_proj, preferred_element_type=jnp.float32)
    pre_up = jnp.dot(chosen, up_proj, preferred_element_type=jnp.float32)
    hidden = (gate * jax.nn.silu(pre_gate) * pre_up).astype(jnp.bfloat16)
    hidden = lax.all_gather(hidden, "local", axis=1, tiled=True)
    contrib = jnp.dot(hidden, down_proj, preferred_element_type=jnp.float32).astype(jnp.bfloat16)
    back = lax.all_to_all(
        contrib.reshape(devices, slots, -1), EVERY, split_axis=0, concat_axis=0, tiled=True
    ).reshape(devices * slots, -1)
    return pl.pallas_call(
        functools.partial(combine_kernel, nodes, locals_, slots),
        out_shape=jax.ShapeDtypeStruct((own_rows, width), jnp.bfloat16),
        name="combine",
    )(expert_ids, back)


def solution(mesh):
    return jax.shard_map(
        on_device,
        mesh=mesh,
        in_specs=(
            P(EVERY, None),
            P(EVERY, None),
            P(EVERY, None),
            P(None, EVERY),
            P(None, EVERY),
            P("node", "local"),
        ),
        out_specs=P(EVERY, None),
        check_vma=False,
    )
```

time: 70.2 us -> 44.1 us (0.63)
  blocking collectives: 31.1 us -> 16.1 us
  starting transfers between devices: 14 us -> 7.4 us
  local copies, waits for them, and re-layouts: 5.2 us -> 0.85 us
  Pallas kernels: 0 us -> 3.54 us
  other arithmetic: 3.32 us -> 0.19 us
  matrix products: 6.06 us -> 4.09 us
  waiting for transfers between devices: 9.91 us -> 11.5 us
    all_gather x3 -> x1, blocking collectives: 18.1 us -> 5.91 us  [on_device(): hidden = lax.all_gather(hidden, 'local', axis=1, tiled=True)]
    all_to_all x3 -> x1, starting transfers between devices: 14 us -> 7.33 us  [on_device(): lax.all_to_all(send, EVERY, split_axis=0, concat_axis=0, tiled=True)]
    pallas_call x0 -> x2, Pallas kernels: none -> 3.54 us  [the longest x1 1.8 us: on_device(): pl.pallas_call(functools.partial(dispatch_kernel, nodes, locals_, slots),...]
    all_to_all x1, blocking collectives: 13 us -> 10.2 us  [on_device(): lax.all_to_all(contrib.reshape(devices, slots, -1), EVERY, split_axis=0,...]
    dot_general x5 -> x3, matrix products: 6.06 us -> 4.09 us  [the longest x1 2.7 us: on_device(): pre_gate = jnp.dot(chosen, gate_proj, preferred_element_type=jnp.float32)]
    gather x3 -> x0, local copies, waits for them, and re-layouts: 1.8 us -> none  [the longest x1 0.62 us: on_device(): compact_rows = jnp.take(flat_rows, source_row, axis=0)]
    ppermute x0 -> x1, waiting for transfers between devices: none -> 1.27 us  [on_device(): other = lax.ppermute(mine, 'local', [(i, i ^ 1) for i in range(locals_)])]
    select_n x6 -> x0, other arithmetic: 0.95 us -> none  [the longest x1 0.7 us: on_device(): node_of = expert_ids // EXP_NODE]
  transfers between devices with their start and end apart: 3 -> 2, of which waited for: 2 -> 2; matrix products, arithmetic and copies ran while one was open for 4% -> 0% of each run, Pallas kernels for 0% -> 0%
where the time goes in v1:
time: 44.1 us; the launch traced here: 43.8 us
  blocking collectives  16.1 us (37%)
  waiting for transfers between devices  11.5 us (26%)
  starting transfers between devices  7.4 us (17%)
  matrix products  4.09 us (9%)
  Pallas kernels  3.54 us (8%)
  local copies, waits for them, and re-layouts  0.85 us (2%)
    all_to_all x1, waiting for transfers between devices, on_device(): lax.all_to_all(send, EVERY, split_axis=0, concat_axis=0, tiled=True)  10.2 us
    all_to_all x1, blocking collectives, on_device(): lax.all_to_all(contrib.reshape(devices, slots, -1), EVERY, split_axis=0,...  10.2 us
    all_to_all x1, starting transfers between devices, on_device(): lax.all_to_all(send, EVERY, split_axis=0, concat_axis=0, tiled=True)  7.33 us
    all_gather x1, blocking collectives, on_device(): hidden = lax.all_gather(hidden, 'local', axis=1, tiled=True)  5.91 us
    dot_general x1, matrix products, on_device(): pre_gate = jnp.dot(chosen, gate_proj, preferred_element_type=jnp.float32)  2.7 us
    pallas_call x1, Pallas kernels, on_device(): pl.pallas_call(functools.partial(dispatch_kernel, nodes, locals_, slots),...  1.8 us
    pallas_call x1, Pallas kernels, on_device(): pl.pallas_call(functools.partial(combine_kernel, nodes, locals_, slots),...  1.74 us
    ppermute x1, waiting for transfers between devices, on_device(): other = lax.ppermute(mine, 'local', [(i, i ^ 1) for i in range(locals_)])  1.27 us
  transfers between devices with their start and end apart: 2, of which 2 were waited for; matrix products, arithmetic and copies ran while one was open for 0% of the time, Pallas kernels for 0%

profile of v1, /device:TPU:0, one launch (start us, length us, event | category | flops | bytes accessed | tf_op | source)
XLA Modules:
  0.0 43.8 jit_solution(10256881473777079831)
XLA Ops:
  0.0 1.8 %dispatch.1 = bf16[32,2,1920]{2,1,0:T(2,128)(2,1)} custom-call(bf16[4,3584]{1,0:T(4,128)(2,1)} %tok_ref.1, s32[4,6]{1,0:T(4,128)} %ids_ref.3, s32[4,6]{1,0:T(4,128)} %codes_ref.1), custom_call_target="tpu_custom_call" | custom-call | tf_op jit(solution)/shard_map/dispatch/pallas_call | solution.py:84
  1.8 7.3 %all-to-all-start = ((bf16[32,2,1920]{2,1,0:T(2,128)(2,1)}), bf16[32,2,1920]{2,1,0:T(2,128)(2,1)S(1)}, u32[]{:S(2)}, u32[]{:S(2)}) async-start(bf16[32,2,1920]{2,1,0:T(2,128)(2,1)} %dispatch.1), calls=%async_computation | async-start | bytes 491520 | tf_op jit(solution)/shard_map/all_to_all | solution.py:89
  9.2 10.2 %all-to-all-done = bf16[32,2,1920]{2,1,0:T(2,128)(2,1)S(1)} async-done(((bf16[32,2,1920]{2,1,0:T(2,128)(2,1)}), bf16[32,2,1920]{2,1,0:T(2,128)(2,1)S(1)}, u32[]{:S(2)}, u32[]{:S(2)}) %all-to-all-start) | async-done | bytes 245792 | tf_op jit(solution)/shard_map/all_to_all | solution.py:89
  19.4 0.1 reshape.10
  19.5 0.0 copy-start.1
  19.5 0.1 collective-permute-start
  19.6 0.2 fusion.3
  19.8 1.3 %collective-permute-done = bf16[64,1792]{1,0:T(8,128)(2,1)S(1)} collective-permute-done((bf16[64,1792]{1,0:T(8,128)(2,1)S(1)}, bf16[64,1792]{1,0:T(8,128)(2,1)S(1)}, u32[]{:S(2)}, u32[]{:S(2)}) %collective-permute-start) | collective-permute-done | bytes 229408 | tf_op jit(solution)/shard_map/ppermute | solution.py:92
  21.1 2.7 %fusion.1 = f32[64,512]{1,0:T(8,128)S(1)} fusion(bf16[3584,512]{1,0:T(8,128)(2,1)} %param.9, bf16[64,1792]{1,0:T(8,128)(2,1)S(1)} %collective-permute-done, bf16[64,1792]{1,0:T(8,128)(2,1)S(1)} %slice.29, pred[]{:T(512)S(6)} %eq.13), kind=kOutput, calls=%fused_computation.4 | convolution fusion | flops 236945408 | bytes 4259841 | tf_op jit(solution)/shard_map/dot_general | solution.py:105
  23.8 0.0 copy-done.1
  23.8 0.0 copy-start
  23.8 0.7 %fusion = bf16[64,512]{1,0:T(8,128)(2,1)S(1)} fusion(bf16[3584,512]{1,0:T(8,128)(2,1)S(1)} %copy-done.1, f32[64,512]{1,0:T(8,128)S(1)} %fusion.1, bf16[64,1792]{1,0:T(8,128)(2,1)S(1)} %collective-permute-done, bf16[64,1792]{1,0:T(8,128)(2,1)S(1)} %slice.29, pred[]{:T(512)S(6)} %eq.13, f32[64]{0:T(128)S(1)} %fusion.3), kind=kOutput, calls=%fused_computation.2 | convolution fusion | flops 237174784 | bytes 4325633 | tf_op jit(solution)/shard_map/dot_general | solution.py:106
  24.5 5.9 %all_gather.3 = bf16[64,2048]{1,0:T(8,128)(2,1)S(1)} all-gather(bf16[64,512]{1,0:T(8,128)(2,1)S(1)} %fusion), channel_id=1, replica_groups=mesh['node'=8,'local'=4] {'local'}, dimensions={1}, use_global_device_ids=true | all-gather | bytes 327680 | tf_op jit(solution)/shard_map/all_gather | solution.py:108
  30.4 0.0 copy-done
  30.4 0.7 %convolution_convert_fusion = bf16[64,896]{1,0:T(8,128)(2,1)S(1)} fusion(bf16[64,2048]{1,0:T(8,128)(2,1)S(1)} %all_gather.3, bf16[2048,896]{1,0:T(8,128)(2,1)S(1)} %copy-done), kind=kOutput, calls=%fused_computation | convolution fusion | flops 234938368 | bytes 4046848 | tf_op jit(solution)/shard_map/dot_general | solution.py:109
  31.2 10.2 %all_to_all.10 = bf16[32,2,896]{2,1,0:T(2,128)(2,1)S(1)} all-to-all(bf16[32,2,896]{2,1,0:T(2,128)(2,1)S(1)} %reshape.11), channel_id=1, replica_groups=mesh['node'=8,'local'=4] {'node','local'}, dimensions={0} | all-to-all | bytes 229376 | tf_op jit(solution)/shard_map/all_to_all | solution.py:110
  41.3 0.7 %reshape.12.back_ref = bf16[64,896]{1,0:T(8,128)(2,1)} reshape(bf16[32,2,896]{2,1,0:T(2,128)(2,1)S(1)} %all_to_all.10) | data formatting | bytes 229376 | tf_op jit(solution)/shard_map/reshape | solution.py:112
  42.0 1.7 %combine.1 = bf16[4,3584]{1,0:T(4,128)(2,1)} custom-call(s32[4,6]{1,0:T(4,128)} %ids_ref.3, bf16[64,896]{1,0:T(8,128)(2,1)} %reshape.12.back_ref), custom_call_target="tpu_custom_call" | custom-call | tf_op jit(solution)/shard_map/combine/pallas_call | solution.py:113
  (3 shorter events, 0.1 us)
Async XLA Ops:
  1.8 17.6 %all-to-all-start = ((bf16[32,2,1920]{2,1,0:T(2,128)(2,1)}), bf16[32,2,1920]{2,1,0:T(2,128)(2,1)S(1)}, u32[]{:S(2)}, u32[]{:S(2)}) async-start(bf16[32,2,1920]{2,1,0:T(2,128)(2,1)} %dispatch.1), calls=%async_computation | async-start | bytes 491520 | tf_op jit(solution)/shard_map/all_to_all | solution.py:89
  19.5 4.3 %copy-start.1 = (bf16[3584,512]{1,0:T(8,128)(2,1)S(1)}, bf16[3584,512]{1,0:T(8,128)(2,1)}, u32[]{:S(2)}) copy-start(bf16[3584,512]{1,0:T(8,128)(2,1)} %param.10) | copy-start | bytes 11010052
  19.5 1.6 %collective-permute-start = (bf16[64,1792]{1,0:T(8,128)(2,1)S(1)}, bf16[64,1792]{1,0:T(8,128)(2,1)S(1)}, u32[]{:S(2)}, u32[]{:S(2)}) collective-permute-start(bf16[64,1792]{1,0:T(8,128)(2,1)S(1)} %slice.29), channel_id=1, source_target_pairs={{0,1},{1,0},{2,3},{3,2},{4,5},{5,4},{6,7},{7,6},{8,9},{9,8},{10,11... | collective-permute-start | bytes 688136 | tf_op jit(solution)/shard_map/ppermute | solution.py:92
  23.8 6.6 %copy-start = (bf16[2048,896]{1,0:T(8,128)(2,1)S(1)}, bf16[2048,896]{1,0:T(8,128)(2,1)}, u32[]{:S(2)}) copy-start(bf16[2048,896]{1,0:T(8,128)(2,1)} %param.11) | copy-start | bytes 11010052

commit v2 on v1

v2 whole, which is shorter than its diff:
```python
import functools

import jax
import jax.numpy as jnp
from jax import lax
from jax.experimental import pallas as pl
from jax.experimental.pallas import tpu as pltpu
from jax.sharding import PartitionSpec as P

FF_E = 1024
EXP_NODE = 2
NL = 4
ROUTE_SCALE = 2.5
LANES = 128
EVERY = ("node", "local")
ANY = pl.BlockSpec(memory_space=pltpu.HBM)
VMEM = pl.BlockSpec(memory_space=pltpu.VMEM)


def small(kib):
    return pltpu.CompilerParams(vmem_limit_bytes=kib << 10)


def resident(array):
    return pltpu.with_memory_space_constraint(array, pltpu.VMEM)


def slot_mask(ids, group, slot):
    rows = ids.shape[0]
    node_of = ids // EXP_NODE
    used = jnp.zeros(group.shape, jnp.bool_)
    for k in range(ids.shape[1]):
        used = used | (node_of[:, k : k + 1] == group)
    used = used.astype(jnp.int32)
    ranks, so_far = [], jnp.zeros((1, group.shape[1]), jnp.int32)
    for t in range(rows):
        ranks.append(so_far)
        so_far = so_far + used[t : t + 1]
    rank = jnp.concatenate(ranks, axis=0)
    return jnp.where((used > 0) & (rank == slot), 1.0, 0.0)


def dispatch_kernel(nodes, lanes_local, slots, tok_hbm, ids_hbm, codes_hbm, out_ref, pick_ref, tok_ref, ids_ref, codes_ref, sems):
    copies = [
        pltpu.make_async_copy(source, target, sems.at[i])
        for i, (source, target) in enumerate(((ids_hbm, ids_ref), (codes_hbm, codes_ref), (tok_hbm, tok_ref)))
    ]
    for copy in copies:
        copy.start()
    copies[0].wait()
    ids = ids_ref[...]
    rows, top = ids.shape
    width = tok_ref.shape[1]
    half = width // 2
    count = nodes * slots
    spot = lax.broadcasted_iota(jnp.int32, (rows, count), 1)
    mask = slot_mask(ids, spot // slots, spot % slots).astype(jnp.bfloat16)
    wide = nodes * lanes_local * slots
    spot = lax.broadcasted_iota(jnp.int32, (rows, wide), 1)
    wide_mask = slot_mask(ids, spot // (lanes_local * slots), spot % slots)
    owner = (spot // slots) % lanes_local
    pick = [jnp.where(owner == l, wide_mask, 0.0) for l in range(lanes_local)]
    pick_ref[...] = jnp.concatenate(pick, axis=0).astype(jnp.bfloat16)
    copies[1].wait()
    codes = codes_ref[...].astype(jnp.float32)
    weight = ROUTE_SCALE * codes / jnp.sum(codes, axis=1, keepdims=True)
    high = weight.astype(jnp.bfloat16).astype(jnp.float32)
    middle = (weight - high).astype(jnp.bfloat16).astype(jnp.float32)
    low = weight - high - middle
    lane = lax.broadcasted_iota(jnp.int32, (rows, LANES), 1)
    score = jnp.zeros((rows, LANES), jnp.float32)
    for part, values in enumerate((ids.astype(jnp.float32), high, middle, low)):
        for k in range(top):
            score = jnp.where(lane == part * top + k, values[:, k : k + 1], score)
    contract = (((0,), (0,)), ((), ()))
    scored = lax.dot_general(
        mask, score.astype(jnp.bfloat16), contract, preferred_element_type=jnp.float32
    ).astype(jnp.bfloat16)
    copies[2].wait()
    placed = lax.dot_general(mask, tok_ref[...], contract, preferred_element_type=jnp.float32).astype(jnp.bfloat16)
    for n in range(nodes):
        own = slice(n * slots, (n + 1) * slots)
        for l in range(lanes_local):
            side = l % 2
            out_ref[n * lanes_local + l, :, :half] = placed[own, side * half : (side + 1) * half]
            out_ref[n * lanes_local + l, :, half:] = scored[own]


def first_kernel(half, mine_ref, gate_ref, up_ref, sum_ref):
    side = lax.axis_index("local") % 2
    part = pl.ds(pl.multiple_of(side * half, half), half)
    width = gate_ref.shape[1]
    mine = mine_ref[:, :, :half].reshape(sum_ref.shape[0], half)
    sum_ref[:, :width] = jnp.dot(mine, gate_ref[part, :], preferred_element_type=jnp.float32)
    sum_ref[:, width:] = jnp.dot(mine, up_ref[part, :], preferred_element_type=jnp.float32)


def second_kernel(half, top, sum_ref, mine_ref, other_ref, gate_ref, up_ref, hidden_ref):
    local = lax.axis_index("local")
    side = 1 - local % 2
    part = pl.ds(pl.multiple_of(side * half, half), half)
    width = gate_ref.shape[1]
    expert = lax.axis_index("node") * EXP_NODE + local * width // FF_E
    rows = sum_ref.shape[0]
    score = mine_ref[:, :, half:].reshape(rows, LANES).astype(jnp.float32)
    named = score[:, :top] == expert.astype(jnp.float32)
    weight = score[:, top : 2 * top] + score[:, 2 * top : 3 * top] + score[:, 3 * top : 4 * top]
    scale = jnp.sum(jnp.where(named, weight, 0.0), axis=1, keepdims=True)
    other = other_ref[:, :, :half].reshape(rows, half)
    pre_gate = sum_ref[:, :width] + jnp.dot(other, gate_ref[part, :], preferred_element_type=jnp.float32)
    pre_up = sum_ref[:, width:] + jnp.dot(other, up_ref[part, :], preferred_element_type=jnp.float32)
    hidden_ref[...] = (scale * (pre_gate / (1.0 + jnp.exp(-pre_gate))) * pre_up).astype(jnp.bfloat16)


def down_near_kernel(mask, *refs):
    count = len(mask)
    pieces, down_ref, sum_ref = refs[:count], refs[count], refs[count + 1]
    local = lax.axis_index("local")
    total = None
    for flip, piece in zip(mask, pieces):
        depth = piece.shape[1]
        part = pl.ds(pl.multiple_of((local ^ flip) * depth, depth), depth)
        term = jnp.dot(piece[...], down_ref[part, :], preferred_element_type=jnp.float32)
        total = term if total is None else total + term
    sum_ref[...] = total


def down_far_kernel(mask, *refs):
    count = len(mask)
    pieces, down_ref, near_ref, out_ref = refs[:count], refs[count], refs[count + 1], refs[count + 2]
    local = lax.axis_index("local")
    total = near_ref[...]
    for flip, piece in zip(mask, pieces):
        depth = piece.shape[1]
        part = pl.ds(pl.multiple_of((local ^ flip) * depth, depth), depth)
        total = total + jnp.dot(piece[...], down_ref[part, :], preferred_element_type=jnp.float32)
    out_ref[...] = total.astype(jnp.bfloat16).reshape(out_ref.shape)


def combine_kernel(lanes_local, pick_ref, back_ref, out_ref):
    devices, slots, piece = back_ref.shape
    rows = out_ref.shape[0]
    summed = jnp.dot(
        pick_ref[...], back_ref[...].reshape(devices * slots, piece), preferred_element_type=jnp.float32
    ).astype(jnp.bfloat16)
    for l in range(lanes_local):
        out_ref[:, l * piece : (l + 1) * piece] = summed[l * rows : (l + 1) * rows]


def on_device(tokens, expert_ids, gate_codes, gate_proj, up_proj, down_proj):
    nodes, locals_ = lax.axis_size("node"), lax.axis_size("local")
    own_rows, width = tokens.shape
    top = expert_ids.shape[1]
    slots = -(-(own_rows * NL) // nodes)
    devices = nodes * locals_
    half = width // 2
    total_rows = devices * slots
    send, pick = pl.pallas_call(
        functools.partial(dispatch_kernel, nodes, locals_, slots),
        out_shape=(
            jax.ShapeDtypeStruct((devices, slots, half + LANES), jnp.bfloat16),
            jax.ShapeDtypeStruct((locals_ * own_rows, total_rows), jnp.bfloat16),
        ),
        in_specs=[ANY] * 3,
        out_specs=(VMEM, VMEM),
        scratch_shapes=[
            pltpu.VMEM(tokens.shape, tokens.dtype),
            pltpu.VMEM(expert_ids.shape, expert_ids.dtype),
            pltpu.VMEM(gate_codes.shape, gate_codes.dtype),
            pltpu.SemaphoreType.DMA((3,)),
        ],
        compiler_params=small(4096),
        cost_estimate=pl.CostEstimate(flops=10**10, bytes_accessed=40 << 20, transcendentals=0),
        name="dispatch",
    )(*(pltpu.with_memory_space_constraint(a, pltpu.HBM) for a in (tokens, expert_ids, gate_codes)))
    arrived = lax.all_to_all(send, EVERY, split_axis=0, concat_axis=0, tiled=True)
    flip = lambda array, bit: lax.ppermute(array, "local", [(i, i ^ bit) for i in range(locals_)])
    other = flip(arrived, 1)

    per_lane = gate_proj.shape[1]
    sums = pl.pallas_call(
        functools.partial(first_kernel, half),
        out_shape=jax.ShapeDtypeStruct((total_rows, 2 * per_lane), jnp.float32),
        in_specs=[VMEM] + [pl.BlockSpec()] * 2,
        out_specs=VMEM,
        compiler_params=small(16384),
        name="first",
    )(arrived, gate_proj, up_proj)
    hidden = pl.pallas_call(
        functools.partial(second_kernel, half, top),
        out_shape=jax.ShapeDtypeStruct((total_rows, per_lane), jnp.bfloat16),
        in_specs=[VMEM] * 3 + [pl.BlockSpec()] * 2,
        out_specs=VMEM,
        compiler_params=small(16384),
        name="second",
    )(sums, arrived, other, gate_proj, up_proj)
    bits = [1 << b for b in range(1, locals_.bit_length() - 1)]
    far = {0: hidden}
    for bit in reversed(bits):
        far.update({key ^ bit: flip(piece, bit) for key, piece in list(far.items())})
    near_mask = (0, 1)
    near_pieces = (hidden, flip(hidden, 1))
    near = pl.pallas_call(
        functools.partial(down_near_kernel, near_mask),
        out_shape=jax.ShapeDtypeStruct((total_rows, down_proj.shape[1]), jnp.float32),
        in_specs=[VMEM] + [pl.BlockSpec()] * 2,
        out_specs=VMEM,
        compiler_params=small(16384),
        cost_estimate=pl.CostEstimate(flops=10**9, bytes_accessed=4 << 20, transcendentals=0),
        name="down_near",
    )(*near_pieces, down_proj)
    far.pop(0)
    keys = list(far)
    far_mask = tuple(keys) + tuple(key ^ 1 for key in keys)
    far_pieces = [far[key] for key in keys]
    far_pieces = far_pieces + [flip(piece, 1) for piece in far_pieces]
    contrib = pl.pallas_call(
        functools.partial(down_far_kernel, far_mask),
        out_shape=jax.ShapeDtypeStruct((devices, slots, down_proj.shape[1]), jnp.bfloat16),
        in_specs=[VMEM] * (len(far_mask) + 2),
        out_specs=VMEM,
        compiler_params=small(16384),
        name="down_far",
    )(*far_pieces, down_proj, near)
    back = lax.all_to_all(contrib, EVERY, split_axis=0, concat_axis=0, tiled=True)
    return pl.pallas_call(
        functools.partial(combine_kernel, locals_),
        out_shape=jax.ShapeDtypeStruct((own_rows, width), jnp.bfloat16),
        in_specs=[VMEM] * 2,
        out_specs=VMEM,
        compiler_params=small(4096),
        name="combine",
    )(pick, back)


def solution(mesh):
    return jax.shard_map(
        on_device,
        mesh=mesh,
        in_specs=(
            P(EVERY, None),
            P(EVERY, None),
            P(EVERY, None),
            P(None, EVERY),
            P(None, EVERY),
            P("node", "local"),
        ),
        out_specs=P(EVERY, None),
        check_vma=False,
    )
```

time: 44.1 us -> 38.2 us (0.87)
  blocking collectives: 16.1 us -> 27.6 us
  starting transfers between devices: 7.4 us -> 0.59 us
  waiting for transfers between devices: 11.5 us -> 5.28 us
  matrix products: 4.09 us -> 0 us
  Pallas kernels: 3.54 us -> 4.57 us
  local copies, waits for them, and re-layouts: 0.85 us -> 0.01 us
    all_to_all x1 -> x2, blocking collectives: 10.2 us -> 27.6 us  [the longest x1 17.4 us: on_device(): lax.all_to_all(send, EVERY, split_axis=0, concat_axis=0, tiled=True)]
    all_to_all x1 -> x0, waiting for transfers between devices: 10.2 us -> none  [on_device(): lax.all_to_all(send, EVERY, split_axis=0, concat_axis=0, tiled=True)]
    all_to_all x1 -> x0, starting transfers between devices: 7.33 us -> none  [on_device(): lax.all_to_all(send, EVERY, split_axis=0, concat_axis=0, tiled=True)]
    all_gather x1 -> x0, blocking collectives: 5.91 us -> none  [on_device(): hidden = lax.all_gather(hidden, 'local', axis=1, tiled=True)]
    dot_general x3 -> x0, matrix products: 4.09 us -> none  [the longest x1 2.7 us: on_device(): pre_gate = jnp.dot(chosen, gate_proj, preferred_element_type=jnp.float32)]
    ppermute x1 -> x4, waiting for transfers between devices: 1.27 us -> 5.28 us  [on_device(): lax.ppermute(array, 'local', [(i, i ^ bit) for i in range(locals_)])]
    pallas_call x1 -> x5, Pallas kernels: 1.74 us -> 3.13 us  [the longest x1 0.76 us: on_device(): pl.pallas_call(functools.partial(second_kernel, half, top), out_shape=jax...]
    reshape x3 -> x0, local copies, waits for them, and re-layouts: 0.82 us -> none  [the longest x1 0.68 us: on_device(): back = lax.all_to_all(contrib.reshape(devices, slots, -1), EVERY, split_a...]
  transfers between devices with their start and end apart: 2 -> 4, of which waited for: 2 -> 3; matrix products, arithmetic and copies ran while one was open for 0% -> 0% of each run, Pallas kernels for 0% -> 3%
where the time goes in v2:
time: 38.2 us; the launch traced here: 38.1 us
  blocking collectives  27.6 us (72%)
  waiting for transfers between devices  5.28 us (14%)
  Pallas kernels  4.57 us (12%)
  starting transfers between devices  0.59 us (2%)
    all_to_all x1, blocking collectives, on_device(): lax.all_to_all(send, EVERY, split_axis=0, concat_axis=0, tiled=True)  17.4 us
    all_to_all x1, blocking collectives, on_device(): lax.all_to_all(contrib, EVERY, split_axis=0, concat_axis=0, tiled=True)  10.2 us
    ppermute x4, waiting for transfers between devices, on_device(): lax.ppermute(array, 'local', [(i, i ^ bit) for i in range(locals_)])  5.28 us
    pallas_call x1, Pallas kernels, on_device(): pl.pallas_call(functools.partial(dispatch_kernel, nodes, locals_, slots),...  1.44 us
  transfers between devices with their start and end apart: 4, of which 3 were waited for; matrix products, arithmetic and copies ran while one was open for 0% of the time, Pallas kernels for 3%

profile of v2, /device:TPU:0, one launch (start us, length us, event | category | flops | bytes accessed | tf_op | source)
XLA Modules:
  0.0 38.1 jit_solution(14450885857974989948)
XLA Ops:
  0.0 0.0 copy-start.1
  0.0 0.0 copy-start
  0.0 1.4 %dispatch.1 = (bf16[32,2,1920]{2,1,0:T(2,128)(2,1)S(1)}, bf16[16,64]{1,0:T(8,128)(2,1)S(1)}) custom-call(bf16[4,3584]{1,0:T(4,128)(2,1)} %tok_hbm.1, s32[4,6]{1,0:T(4,128)} %ids_hbm.1, s32[4,6]{1,0:T(4,128)} %codes_hbm.1), custom_call_target="tpu_custom_call" | custom-call | flops 10000000000 | bytes 41943040 | tf_op jit(solution)/shard_map/dispatch/pallas_call | solution.py:158
  1.4 17.4 %all_to_all.10.mine_ref = bf16[32,2,1920]{2,1,0:T(2,128)(2,1)S(1)} all-to-all(bf16[32,2,1920]{2,1,0:T(2,128)(2,1)S(1)} %get-tuple-element.8), channel_id=1, replica_groups=mesh['node'=8,'local'=4] {'node','local'}, dimensions={0} | all-to-all | bytes 491520 | tf_op jit(solution)/shard_map/all_to_all | solution.py:176
  18.8 0.0 collective-permute-start
  18.8 0.0 copy-done.1
  18.8 0.0 copy-done
  18.9 0.8 %first.1.sum_ref = f32[64,1024]{1,0:T(8,128)S(1)} custom-call(bf16[32,2,1920]{2,1,0:T(2,128)(2,1)S(1)} %all_to_all.10.mine_ref, bf16[3584,512]{1,0:T(8,128)(2,1)S(1)} %copy-done, bf16[3584,512]{1,0:T(8,128)(2,1)S(1)} %copy-done.1), custom_call_target="tpu_custom_call" | custom-call | tf_op jit(solution)/shard_map/first/pallas_call | solution.py:181
  19.6 0.0 copy-start.2
  19.6 0.7 %collective-permute-done.other_ref = bf16[32,2,1920]{2,1,0:T(2,128)(2,1)S(1)} collective-permute-done((bf16[32,2,1920]{2,1,0:T(2,128)(2,1)S(1)}, bf16[32,2,1920]{2,1,0:T(2,128)(2,1)S(1)}, u32[]{:S(2)}, u32[]{:S(2)}) %collective-permute-start) | collective-permute-done | bytes 245792 | tf_op jit(solution)/shard_map/ppermute | solution.py:177
  20.4 0.8 %second.1.refs_0_ = bf16[64,512]{1,0:T(8,128)(2,1)S(1)} custom-call(f32[64,1024]{1,0:T(8,128)S(1)} %first.1.sum_ref, bf16[32,2,1920]{2,1,0:T(2,128)(2,1)S(1)} %all_to_all.10.mine_ref, bf16[32,2,1920]{2,1,0:T(2,128)(2,1)S(1)} %collective-permute-done.other_ref, bf16[3584,512]{1,0:T(8,128)(2,1)S(1)} %copy-done, bf16[3584,512]{1,0:T(8,128)(2,1)S(1)} %copy-done.1), custom_call_target="tpu_custom_call" | custom-call | tf_op jit(solution)/shard_map/second/pallas_call | solution.py:189
  21.1 0.5 %collective-permute-start.1 = (bf16[64,512]{1,0:T(8,128)(2,1)S(1)}, bf16[64,512]{1,0:T(8,128)(2,1)S(1)}, u32[]{:S(2)}, u32[]{:S(2)}) collective-permute-start(bf16[64,512]{1,0:T(8,128)(2,1)S(1)} %second.1.refs_0_), channel_id=1, source_target_pairs={{0,2},{1,3},{2,0},{3,1},{4,6},{5,7},{6,4},{7,5},{8,10},{9,11},{10,... | collective-permute-start | bytes 196616 | tf_op jit(solution)/shard_map/ppermute | solution.py:177
  21.6 0.1 collective-permute-start.3
  21.7 3.7 %collective-permute-done.1.refs_0_ = bf16[64,512]{1,0:T(8,128)(2,1)S(1)} collective-permute-done((bf16[64,512]{1,0:T(8,128)(2,1)S(1)}, bf16[64,512]{1,0:T(8,128)(2,1)S(1)}, u32[]{:S(2)}, u32[]{:S(2)}) %collective-permute-start.1) | collective-permute-done | bytes 65568 | tf_op jit(solution)/shard_map/ppermute | solution.py:177
  25.5 0.0 collective-permute-start.2
  25.5 0.0 collective-permute-done.3.refs_1_
  25.5 0.0 copy-done.2
  25.5 0.4 %down_near.1.refs_3_ = f32[64,896]{1,0:T(8,128)S(1)} custom-call(bf16[64,512]{1,0:T(8,128)(2,1)S(1)} %second.1.refs_0_, bf16[64,512]{1,0:T(8,128)(2,1)S(1)} %collective-permute-done.3.refs_1_, bf16[2048,896]{1,0:T(8,128)(2,1)S(1)} %copy-done.2), custom_call_target="tpu_custom_call" | custom-call | flops 1000000000 | bytes 4194304 | tf_op jit(solution)/shard_map/down_near/pallas_call | solution.py:203
  25.9 0.8 %collective-permute-done.2.refs_1_ = bf16[64,512]{1,0:T(8,128)(2,1)S(1)} collective-permute-done((bf16[64,512]{1,0:T(8,128)(2,1)S(1)}, bf16[64,512]{1,0:T(8,128)(2,1)S(1)}, u32[]{:S(2)}, u32[]{:S(2)}) %collective-permute-start.2) | collective-permute-done | bytes 65568 | tf_op jit(solution)/shard_map/ppermute | solution.py:177
  26.7 0.4 %down_far.1 = bf16[32,2,896]{2,1,0:T(2,128)(2,1)S(1)} custom-call(bf16[64,512]{1,0:T(8,128)(2,1)S(1)} %collective-permute-done.1.refs_0_, bf16[64,512]{1,0:T(8,128)(2,1)S(1)} %collective-permute-done.2.refs_1_, bf16[2048,896]{1,0:T(8,128)(2,1)S(1)} %copy-done.2, f32[64,896]{1,0:T(8,128)S(1)} %down_near.1.refs_3_), custom_call_target="tpu_custom_call" | custom-call | tf_op jit(solution)/shard_map/down_far/pallas_call | solution.py:217
  27.2 10.2 %all_to_all.11.back_ref = bf16[32,2,896]{2,1,0:T(2,128)(2,1)S(1)} all-to-all(bf16[32,2,896]{2,1,0:T(2,128)(2,1)S(1)} %down_far.1), channel_id=1, replica_groups=mesh['node'=8,'local'=4] {'node','local'}, dimensions={0} | all-to-all | bytes 229376 | tf_op jit(solution)/shard_map/all_to_all | solution.py:225
  37.3 0.8 %combine.1 = bf16[4,3584]{1,0:T(4,128)(2,1)} custom-call(bf16[16,64]{1,0:T(8,128)(2,1)S(1)} %get-tuple-element.7.pick_ref, bf16[32,2,896]{2,1,0:T(2,128)(2,1)S(1)} %all_to_all.11.back_ref), custom_call_target="tpu_custom_call" | custom-call | tf_op jit(solution)/shard_map/combine/pallas_call | solution.py:226
Async XLA Ops:
  0.0 18.8 %copy-start.1 = (bf16[3584,512]{1,0:T(8,128)(2,1)S(1)}, bf16[3584,512]{1,0:T(8,128)(2,1)}, u32[]{:S(2)}) copy-start(bf16[3584,512]{1,0:T(8,128)(2,1)} %up_ref.3) | copy-start | bytes 11010052
  0.0 18.8 %copy-start = (bf16[3584,512]{1,0:T(8,128)(2,1)S(1)}, bf16[3584,512]{1,0:T(8,128)(2,1)}, u32[]{:S(2)}) copy-start(bf16[3584,512]{1,0:T(8,128)(2,1)} %gate_ref.3) | copy-start | bytes 11010052
  18.8 1.5 %collective-permute-start = (bf16[32,2,1920]{2,1,0:T(2,128)(2,1)S(1)}, bf16[32,2,1920]{2,1,0:T(2,128)(2,1)S(1)}, u32[]{:S(2)}, u32[]{:S(2)}) collective-permute-start(bf16[32,2,1920]{2,1,0:T(2,128)(2,1)S(1)} %all_to_all.10.mine_ref), channel_id=1, source_target_pairs={{0,1},{1,0},{2,3},{3,2},{4,5},{5,4},{6,7},{7,6},{8,9},{9,8},{10,11... | collective-permute-start | bytes 737288 | tf_op jit(solution)/shard_map/ppermute | solution.py:177
  19.6 5.8 %copy-start.2 = (bf16[2048,896]{1,0:T(8,128)(2,1)S(1)}, bf16[2048,896]{1,0:T(8,128)(2,1)}, u32[]{:S(2)}) copy-start(bf16[2048,896]{1,0:T(8,128)(2,1)} %refs_2_.3) | copy-start | bytes 11010052
  21.1 4.3 %collective-permute-start.1 = (bf16[64,512]{1,0:T(8,128)(2,1)S(1)}, bf16[64,512]{1,0:T(8,128)(2,1)S(1)}, u32[]{:S(2)}, u32[]{:S(2)}) collective-permute-start(bf16[64,512]{1,0:T(8,128)(2,1)S(1)} %second.1.refs_0_), channel_id=1, source_target_pairs={{0,2},{1,3},{2,0},{3,1},{4,6},{5,7},{6,4},{7,5},{8,10},{9,11},{10,... | collective-permute-start | bytes 196616 | tf_op jit(solution)/shard_map/ppermute | solution.py:177
  21.6 3.9 %collective-permute-start.3 = (bf16[64,512]{1,0:T(8,128)(2,1)S(1)}, bf16[64,512]{1,0:T(8,128)(2,1)S(1)}, u32[]{:S(2)}, u32[]{:S(2)}) collective-permute-start(bf16[64,512]{1,0:T(8,128)(2,1)S(1)} %second.1.refs_0_), channel_id=1, source_target_pairs={{0,1},{1,0},{2,3},{3,2},{4,5},{5,4},{6,7},{7,6},{8,9},{9,8},{10,11... | collective-permute-start | bytes 196616 | tf_op jit(solution)/shard_map/ppermute | solution.py:177
  25.5 1.3 %collective-permute-start.2 = (bf16[64,512]{1,0:T(8,128)(2,1)S(1)}, bf16[64,512]{1,0:T(8,128)(2,1)S(1)}, u32[]{:S(2)}, u32[]{:S(2)}) collective-permute-start(bf16[64,512]{1,0:T(8,128)(2,1)S(1)} %collective-permute-done.1.refs_0_), channel_id=1, source_target_pairs={{0,1},{1,0},{2,3},{3,2},{4,5},{5,4},{6,7},{7,6},{8,9},{9,8},{10,11... | collective-permute-start | bytes 196616 | tf_op jit(solution)/shard_map/ppermute | solution.py:177

commit v3 on v2

v3 whole, which is shorter than its diff:
```python
import functools

import jax
import jax.numpy as jnp
from jax import lax
from jax.experimental import pallas as pl
from jax.experimental.pallas import tpu as pltpu
from jax.sharding import PartitionSpec as P


FF_E = 1024
EXP_NODE = 2
NL = 4
ROUTE_SCALE = 2.5
LANES = 128
CODE_BASE = 32
EVERY = ("node", "local")
HBM = pl.BlockSpec(memory_space=pltpu.HBM)
VMEM = pl.BlockSpec(memory_space=pltpu.VMEM)


def small(kib):
    return pltpu.CompilerParams(vmem_limit_bytes=kib << 10)


def split(index, size):
    whole = jnp.floor((index + 0.5) / size)
    return whole, index - whole * size


def slot_mask(ids, group, slot):
    lowest = group * EXP_NODE
    used = None
    for k in range(ids.shape[1]):
        offset = ids[:, k : k + 1] - lowest
        hit = (offset >= 0.0) & (offset < EXP_NODE)
        used = hit if used is None else used | hit
    used = jnp.where(used, 1.0, 0.0)
    ranks, so_far = [], jnp.zeros((1, group.shape[1]), jnp.float32)
    for t in range(ids.shape[0]):
        ranks.append(so_far)
        so_far = so_far + used[t : t + 1]
    return jnp.where(jnp.concatenate(ranks, axis=0) == slot, used, 0.0)


def pick_kernel(nodes, lanes_local, slots, ids_ref, pick_ref):
    ids = ids_ref[...].astype(jnp.float32)
    spot = lax.broadcasted_iota(jnp.int32, (ids.shape[0], nodes * lanes_local * slots), 1).astype(jnp.float32)
    device, slot = split(spot, slots)
    group, owner = split(device, lanes_local)
    mask = slot_mask(ids, group, slot)
    pick = [jnp.where(owner == l, mask, 0.0) for l in range(lanes_local)]
    pick_ref[...] = jnp.concatenate(pick, axis=0).astype(jnp.bfloat16)


def dispatch_kernel(nodes, lanes_local, slots, tok_hbm, ids_hbm, codes_hbm, out_ref, tok_ref, ids_ref, codes_ref, sems):
    copies = [
        pltpu.make_async_copy(source, target, sems.at[i])
        for i, (source, target) in enumerate(((ids_hbm, ids_ref), (codes_hbm, codes_ref), (tok_hbm, tok_ref)))
    ]
    for copy in copies:
        copy.start()
    copies[0].wait()
    rows, top = ids_ref.shape
    half = tok_ref.shape[1] // 2
    ids = ids_ref[...].astype(jnp.float32)
    spot = lax.broadcasted_iota(jnp.int32, (rows, nodes * slots), 1).astype(jnp.float32)
    mask = slot_mask(ids, *split(spot, slots)).astype(jnp.bfloat16)
    copies[1].wait()
    high, low = split(codes_ref[...].astype(jnp.float32), CODE_BASE)
    rest = jnp.zeros((rows, LANES - 3 * top), jnp.float32)
    score = jnp.concatenate([ids, high, low, rest], axis=1).astype(jnp.bfloat16)
    contract = (((0,), (0,)), ((), ()))
    scored = lax.dot_general(mask, score, contract, preferred_element_type=jnp.float32).astype(jnp.bfloat16)
    copies[2].wait()
    placed = lax.dot_general(mask, tok_ref[...], contract, preferred_element_type=jnp.float32).astype(jnp.bfloat16)
    for n in range(nodes):
        own = slice(n * slots, (n + 1) * slots)
        for l in range(lanes_local):
            side = l % 2
            out_ref[n * lanes_local + l, :, :half] = placed[own, side * half : (side + 1) * half]
            out_ref[n * lanes_local + l, :, half:] = scored[own]


def first_kernel(half, top, mine_ref, gate_ref, up_ref, sum_ref, scale_ref):
    local = lax.axis_index("local")
    part = pl.ds(pl.multiple_of(local % 2 * half, half), half)
    rows, width = sum_ref.shape[0], gate_ref.shape[1]
    mine = mine_ref[:, :, :half].reshape(rows, half)
    sum_ref[:, :width] = jnp.dot(mine, gate_ref[part, :], preferred_element_type=jnp.float32)
    sum_ref[:, width:] = jnp.dot(mine, up_ref[part, :], preferred_element_type=jnp.float32)
    expert = lax.axis_index("node") * EXP_NODE + local * width // FF_E
    score = mine_ref[:, :, half:].reshape(rows, LANES).astype(jnp.float32)
    codes = score[:, top : 2 * top] * CODE_BASE + score[:, 2 * top : 3 * top]
    named = jnp.where(score[:, :top] == expert.astype(jnp.float32), codes, 0.0)
    total = jnp.sum(codes, axis=1, keepdims=True)
    scale = ROUTE_SCALE * jnp.sum(named, axis=1, keepdims=True) / jnp.where(total > 0.0, total, 1.0)
    scale_ref[...] = jnp.broadcast_to(scale, scale_ref.shape)


def second_kernel(half, sum_ref, scale_ref, other_ref, gate_ref, up_ref, hidden_ref):
    local = lax.axis_index("local")
    part = pl.ds(pl.multiple_of((1 - local % 2) * half, half), half)
    rows, width = sum_ref.shape[0], gate_ref.shape[1]
    other = other_ref[:, :, :half].reshape(rows, half)
    if rows < LANES:
        other = jnp.concatenate([other, other], axis=0)
    pre_gate = jnp.dot(other, gate_ref[part, :], preferred_element_type=jnp.float32)
    pre_up = jnp.dot(other, up_ref[part, :], preferred_element_type=jnp.float32)
    pre_gate = sum_ref[:, :width] + pre_gate[:rows]
    pre_up = sum_ref[:, width:] + pre_up[:rows]
    scale = scale_ref[:, :1]
    hidden_ref[...] = (scale * (pre_gate / (1.0 + jnp.exp(-pre_gate))) * pre_up).astype(jnp.bfloat16)


def down_kernel(flips, adds, *refs):
    count = len(flips)
    pieces, down_ref, out_ref = refs[:count], refs[count], refs[-1]
    local = lax.axis_index("local")
    total = refs[count + 1][...] if adds else None
    for flip, piece in zip(flips, pieces):
        depth = piece.shape[1]
        part = pl.ds(pl.multiple_of((local ^ flip) * depth, depth), depth)
        term = jnp.dot(piece[...], down_ref[part, :], preferred_element_type=jnp.float32)
        total = term if total is None else total + term
    out_ref[...] = total.astype(out_ref.dtype).reshape(out_ref.shape)


def combine_kernel(lanes_local, pick_ref, back_ref, out_ref):
    devices, slots, piece = back_ref.shape
    rows = out_ref.shape[0]
    summed = jnp.dot(
        pick_ref[...], back_ref[...].reshape(devices * slots, piece), preferred_element_type=jnp.float32
    ).astype(jnp.bfloat16)
    for l in range(lanes_local):
        out_ref[:, l * piece : (l + 1) * piece] = summed[l * rows : (l + 1) * rows]


def hbm(*arrays):
    return tuple(pltpu.with_memory_space_constraint(array, pltpu.HBM) for array in arrays)


def layer(tokens, expert_ids, gate_codes, gate_proj, up_proj, down_proj):
    nodes, locals_ = lax.axis_size("node"), lax.axis_size("local")
    own_rows, width = tokens.shape
    top = expert_ids.shape[1]
    slots = -(-(own_rows * NL) // nodes)
    devices = nodes * locals_
    half = width // 2
    rows = devices * slots
    per_lane, out_width = gate_proj.shape[1], down_proj.shape[1]
    send = pl.pallas_call(
        functools.partial(dispatch_kernel, nodes, locals_, slots),
        out_shape=jax.ShapeDtypeStruct((devices, slots, half + LANES), jnp.bfloat16),
        in_specs=[HBM] * 3,
        out_specs=VMEM,
        scratch_shapes=[
            pltpu.VMEM(tokens.shape, tokens.dtype),
            pltpu.VMEM(expert_ids.shape, expert_ids.dtype),
            pltpu.VMEM(gate_codes.shape, gate_codes.dtype),
            pltpu.SemaphoreType.DMA((3,)),
        ],
        compiler_params=small(4096),
        cost_estimate=pl.CostEstimate(flops=10**10, bytes_accessed=40 << 20, transcendentals=0),
        name="dispatch",
    )(*hbm(tokens, expert_ids, gate_codes))
    arrived = lax.all_to_all(send, EVERY, split_axis=0, concat_axis=0, tiled=True)

    def flip(array, bit):
        return lax.ppermute(array, "local", [(i, i ^ bit) for i in range(locals_)])

    other = flip(arrived, 1)
    sums, scale = pl.pallas_call(
        functools.partial(first_kernel, half, top),
        out_shape=(
            jax.ShapeDtypeStruct((rows, 2 * per_lane), jnp.float32),
            jax.ShapeDtypeStruct((rows, LANES), jnp.float32),
        ),
        in_specs=[VMEM] + [pl.BlockSpec()] * 2,
        out_specs=(VMEM, VMEM),
        compiler_params=small(16384),
        name="first",
    )(arrived, gate_proj, up_proj)
    hidden = pl.pallas_call(
        functools.partial(second_kernel, half),
        out_shape=jax.ShapeDtypeStruct((rows, per_lane), jnp.bfloat16),
        in_specs=[VMEM] * 3 + [pl.BlockSpec()] * 2,
        out_specs=VMEM,
        compiler_params=small(16384),
        name="second",
    )(sums, scale, other, gate_proj, up_proj)

    def down(pieces, near=None, out=None):
        extra = () if near is None else (near,)
        return pl.pallas_call(
            functools.partial(down_kernel, tuple(pieces), near is not None),
            out_shape=out or jax.ShapeDtypeStruct((rows, out_width), jnp.float32),
            in_specs=[VMEM] * (len(pieces) + 1 + len(extra)),
            out_specs=VMEM,
            compiler_params=small(16384),
            cost_estimate=pl.CostEstimate(
                flops=2 * len(pieces) * rows * per_lane * out_width,
                bytes_accessed=2 * len(pieces) * per_lane * out_width,
                transcendentals=0,
            ),
        )(*pieces.values(), down_proj, *extra)

    far = {0: hidden}
    for b in reversed(range(1, locals_.bit_length() - 1)):
        for key, piece in list(far.items()):
            far[key ^ (1 << b)] = flip(piece, 1 << b)
    del far[0]
    near = down({0: hidden, 1: flip(hidden, 1)})
    relayed = {key ^ 1: flip(piece, 1) for key, piece in far.items()}
    pick = pl.pallas_call(
        functools.partial(pick_kernel, nodes, locals_, slots),
        out_shape=jax.ShapeDtypeStruct((locals_ * own_rows, rows), jnp.bfloat16),
        in_specs=[VMEM],
        out_specs=VMEM,
        compiler_params=small(4096),
        name="pick",
    )(expert_ids)
    lean = down(far, near)
    contrib = down(relayed, lean, jax.ShapeDtypeStruct((devices, slots, out_width), jnp.bfloat16))
    back = lax.all_to_all(contrib, EVERY, split_axis=0, concat_axis=0, tiled=True)
    return pl.pallas_call(
        functools.partial(combine_kernel, locals_),
        out_shape=jax.ShapeDtypeStruct((own_rows, width), jnp.bfloat16),
        in_specs=[VMEM] * 2,
        out_specs=VMEM,
        compiler_params=small(4096),
        name="combine",
    )(pick, back)


def solution(mesh):
    return jax.shard_map(
        layer,
        mesh=mesh,
        in_specs=(
            P(EVERY, None),
            P(EVERY, None),
            P(EVERY, None),
            P(None, EVERY),
            P(None, EVERY),
            P("node", "local"),
        ),
        out_specs=P(EVERY, None),
        check_vma=False,
    )
```

time: 38.2 us -> 39 us (1.021)
  blocking collectives: 27.6 us -> 17.4 us
  waiting for transfers between devices: 5.28 us -> 12.9 us
  starting transfers between devices: 0.59 us -> 3.16 us
  Pallas kernels: 4.57 us -> 5.25 us
    all_to_all x2 -> x1, blocking collectives: 27.6 us -> 17.4 us  [layer(): lax.all_to_all(send, EVERY, split_axis=0, concat_axis=0, tiled=True)]
    all_to_all x0 -> x1, waiting for transfers between devices: none -> 7.89 us  [layer(): lax.all_to_all(contrib, EVERY, split_axis=0, concat_axis=0, tiled=True)]
    all_to_all x0 -> x1, starting transfers between devices: none -> 2.57 us  [layer(): lax.all_to_all(contrib, EVERY, split_axis=0, concat_axis=0, tiled=True)]
    pallas_call x6 -> x8, Pallas kernels: 4.57 us -> 5.25 us  [the longest x3 1.68 us: down(): pl.pallas_call(functools.partial(down_kernel, tuple(pieces), near is not...]
  transfers between devices with their start and end apart: 4 -> 5, of which waited for: 3 -> 4; matrix products, arithmetic and copies ran while one was open for 0% -> 0% of each run, Pallas kernels for 3% -> 4%
where the time goes in v3:
time: 39 us; the launch traced here: 38.7 us
  blocking collectives  17.4 us (45%)
  waiting for transfers between devices  12.9 us (33%)
  Pallas kernels  5.25 us (13%)
  starting transfers between devices  3.16 us (8%)
    all_to_all x1, blocking collectives, layer(): lax.all_to_all(send, EVERY, split_axis=0, concat_axis=0, tiled=True)  17.4 us
    all_to_all x1, waiting for transfers between devices, layer(): lax.all_to_all(contrib, EVERY, split_axis=0, concat_axis=0, tiled=True)  7.89 us
    ppermute x4, waiting for transfers between devices, flip(): return lax.ppermute(array, 'local', [(i, i ^ bit) for i in range(locals_)])  4.97 us
    all_to_all x1, starting transfers between devices, layer(): lax.all_to_all(contrib, EVERY, split_axis=0, concat_axis=0, tiled=True)  2.57 us
    pallas_call x3, Pallas kernels, down(): pl.pallas_call(functools.partial(down_kernel, tuple(pieces), near is not...  1.68 us
    pallas_call x1, Pallas kernels, layer(): pl.pallas_call(functools.partial(dispatch_kernel, nodes, locals_, slots),...  1.31 us
  transfers between devices with their start and end apart: 5, of which 4 were waited for; matrix products, arithmetic and copies ran while one was open for 0% of the time, Pallas kernels for 4%

profile of v3, /device:TPU:0, one launch (start us, length us, event | category | flops | bytes accessed | tf_op | source)
XLA Modules:
  0.0 38.7 jit_solution(4213133598256112265)
XLA Ops:
  0.0 0.0 copy-start.2
  0.0 0.0 copy-start.1
  0.0 1.3 %dispatch.1 = bf16[32,2,1920]{2,1,0:T(2,128)(2,1)S(1)} custom-call(bf16[4,3584]{1,0:T(4,128)(2,1)} %tok_hbm.1, s32[4,6]{1,0:T(4,128)} %ids_hbm.1, s32[4,6]{1,0:T(4,128)} %codes_hbm.1), custom_call_target="tpu_custom_call" | custom-call | flops 10000000000 | bytes 41943040 | tf_op jit(solution)/shard_map/dispatch/pallas_call | solution.py:152
  1.3 17.4 %all_to_all.10.mine_ref = bf16[32,2,1920]{2,1,0:T(2,128)(2,1)S(1)} all-to-all(bf16[32,2,1920]{2,1,0:T(2,128)(2,1)S(1)} %dispatch.1), channel_id=1, replica_groups=mesh['node'=8,'local'=4] {'node','local'}, dimensions={0} | all-to-all | bytes 491520 | tf_op jit(solution)/shard_map/all_to_all | solution.py:167
  18.7 0.0 collective-permute-start
  18.7 0.0 copy-done.2
  18.7 0.0 copy-done.1
  18.7 0.8 %first.1 = (f32[64,1024]{1,0:T(8,128)S(1)}, f32[64,128]{1,0:T(8,128)S(1)}) custom-call(bf16[32,2,1920]{2,1,0:T(2,128)(2,1)S(1)} %all_to_all.10.mine_ref, bf16[3584,512]{1,0:T(8,128)(2,1)S(1)} %copy-done.1, bf16[3584,512]{1,0:T(8,128)(2,1)S(1)} %copy-done.2), custom_call_target="tpu_custom_call" | custom-call | tf_op jit(solution)/shard_map/first/pallas_call | solution.py:173
  19.5 0.7 %collective-permute-done.other_ref = bf16[32,2,1920]{2,1,0:T(2,128)(2,1)S(1)} collective-permute-done((bf16[32,2,1920]{2,1,0:T(2,128)(2,1)S(1)}, bf16[32,2,1920]{2,1,0:T(2,128)(2,1)S(1)}, u32[]{:S(2)}, u32[]{:S(2)}) %collective-permute-start) | collective-permute-done | bytes 245792 | tf_op jit(solution)/shard_map/ppermute | solution.py:170
  20.2 0.0 copy-start
  20.2 0.7 %second.1.refs_0_ = bf16[64,512]{1,0:T(8,128)(2,1)S(1)} custom-call(f32[64,1024]{1,0:T(8,128)S(1)} %get-tuple-element.7.sum_ref, f32[64,128]{1,0:T(8,128)S(1)} %get-tuple-element.8.scale_ref, bf16[32,2,1920]{2,1,0:T(2,128)(2,1)S(1)} %collective-permute-done.other_ref, bf16[3584,512]{1,0:T(8,128)(2,1)S(1)} %copy-done.1, bf16[3584,512]{1,0:T(8,128)(2,1)S(1)} %copy-done.2), custom_call_target="tpu_custom_call" | custom-call | tf_op jit(solution)/shard_map/second/pallas_call | solution.py:184
  20.9 0.5 %collective-permute-start.1 = (bf16[64,512]{1,0:T(8,128)(2,1)S(1)}, bf16[64,512]{1,0:T(8,128)(2,1)S(1)}, u32[]{:S(2)}, u32[]{:S(2)}) collective-permute-start(bf16[64,512]{1,0:T(8,128)(2,1)S(1)} %second.1.refs_0_), channel_id=1, source_target_pairs={{0,2},{1,3},{2,0},{3,1},{4,6},{5,7},{6,4},{7,5},{8,10},{9,11},{10,... | collective-permute-start | bytes 196616 | tf_op jit(solution)/shard_map/ppermute | solution.py:170
  21.4 0.1 collective-permute-start.3
  21.5 3.7 %collective-permute-done.1.refs_0_ = bf16[64,512]{1,0:T(8,128)(2,1)S(1)} collective-permute-done((bf16[64,512]{1,0:T(8,128)(2,1)S(1)}, bf16[64,512]{1,0:T(8,128)(2,1)S(1)}, u32[]{:S(2)}, u32[]{:S(2)}) %collective-permute-start.1) | collective-permute-done | bytes 65568 | tf_op jit(solution)/shard_map/ppermute | solution.py:170
  25.2 0.0 collective-permute-start.2
  25.2 0.0 collective-permute-done.3.refs_1_
  25.2 0.0 copy-done
  25.2 0.4 %shard_map.64.refs_2_ = f32[64,896]{1,0:T(8,128)S(1)} custom-call(bf16[64,512]{1,0:T(8,128)(2,1)S(1)} %second.1.refs_0_, bf16[64,512]{1,0:T(8,128)(2,1)S(1)} %collective-permute-done.3.refs_1_, bf16[2048,896]{1,0:T(8,128)(2,1)S(1)} %copy-done), custom_call_target="tpu_custom_call" | custom-call | flops 117440512 | bytes 1835008 | tf_op jit(solution)/shard_map/pallas_call | solution.py:195
  25.7 0.0 copy-start.3
  25.7 0.3 shard_map.65.refs_2_
  26.0 0.5 %collective-permute-done.2.refs_0_ = bf16[64,512]{1,0:T(8,128)(2,1)S(1)} collective-permute-done((bf16[64,512]{1,0:T(8,128)(2,1)S(1)}, bf16[64,512]{1,0:T(8,128)(2,1)S(1)}, u32[]{:S(2)}, u32[]{:S(2)}) %collective-permute-start.2) | collective-permute-done | bytes 65568 | tf_op jit(solution)/shard_map/ppermute | solution.py:170
  26.5 0.9 %shard_map.66 = bf16[32,2,896]{2,1,0:T(2,128)(2,1)} custom-call(bf16[64,512]{1,0:T(8,128)(2,1)S(1)} %collective-permute-done.2.refs_0_, bf16[2048,896]{1,0:T(8,128)(2,1)S(1)} %copy-done, f32[64,896]{1,0:T(8,128)S(1)} %shard_map.65.refs_2_), custom_call_target="tpu_custom_call" | custom-call | flops 58720256 | bytes 917504 | tf_op jit(solution)/shard_map/pallas_call | solution.py:195
  27.4 2.6 %all-to-all-start.1 = ((bf16[32,2,896]{2,1,0:T(2,128)(2,1)}), bf16[32,2,896]{2,1,0:T(2,128)(2,1)S(1)}, u32[]{:S(2)}, u32[]{:S(2)}) async-start(bf16[32,2,896]{2,1,0:T(2,128)(2,1)} %shard_map.66), calls=%async_computation.1 | async-start | bytes 229376 | tf_op jit(solution)/shard_map/all_to_all | solution.py:225
  30.0 0.0 copy-done.3
  30.0 0.1 pick.1.pick_ref
  30.1 7.9 %all-to-all-done.1.back_ref = bf16[32,2,896]{2,1,0:T(2,128)(2,1)S(1)} async-done(((bf16[32,2,896]{2,1,0:T(2,128)(2,1)}), bf16[32,2,896]{2,1,0:T(2,128)(2,1)S(1)}, u32[]{:S(2)}, u32[]{:S(2)}) %all-to-all-start.1) | async-done | bytes 114720 | tf_op jit(solution)/shard_map/all_to_all | solution.py:225
  38.0 0.8 %combine.1 = bf16[4,3584]{1,0:T(4,128)(2,1)} custom-call(bf16[16,64]{1,0:T(8,128)(2,1)S(1)} %pick.1.pick_ref, bf16[32,2,896]{2,1,0:T(2,128)(2,1)S(1)} %all-to-all-done.1.back_ref), custom_call_target="tpu_custom_call" | custom-call | tf_op jit(solution)/shard_map/combine/pallas_call | solution.py:226
Async XLA Ops:
  0.0 18.7 %copy-start.2 = (bf16[3584,512]{1,0:T(8,128)(2,1)S(1)}, bf16[3584,512]{1,0:T(8,128)(2,1)}, u32[]{:S(2)}) copy-start(bf16[3584,512]{1,0:T(8,128)(2,1)} %up_ref.3) | copy-start | bytes 11010052
  0.0 18.7 %copy-start.1 = (bf16[3584,512]{1,0:T(8,128)(2,1)S(1)}, bf16[3584,512]{1,0:T(8,128)(2,1)}, u32[]{:S(2)}) copy-start(bf16[3584,512]{1,0:T(8,128)(2,1)} %gate_ref.3) | copy-start | bytes 11010052
  18.7 1.5 %collective-permute-start = (bf16[32,2,1920]{2,1,0:T(2,128)(2,1)S(1)}, bf16[32,2,1920]{2,1,0:T(2,128)(2,1)S(1)}, u32[]{:S(2)}, u32[]{:S(2)}) collective-permute-start(bf16[32,2,1920]{2,1,0:T(2,128)(2,1)S(1)} %all_to_all.10.mine_ref), channel_id=1, source_target_pairs={{0,1},{1,0},{2,3},{3,2},{4,5},{5,4},{6,7},{7,6},{8,9},{9,8},{10,11... | collective-permute-start | bytes 737288 | tf_op jit(solution)/shard_map/ppermute | solution.py:170
  20.2 5.0 %copy-start = (bf16[2048,896]{1,0:T(8,128)(2,1)S(1)}, bf16[2048,896]{1,0:T(8,128)(2,1)}, u32[]{:S(2)}) copy-start(bf16[2048,896]{1,0:T(8,128)(2,1)} %refs_1_.3) | copy-start | bytes 11010052
  20.9 4.3 %collective-permute-start.1 = (bf16[64,512]{1,0:T(8,128)(2,1)S(1)}, bf16[64,512]{1,0:T(8,128)(2,1)S(1)}, u32[]{:S(2)}, u32[]{:S(2)}) collective-permute-start(bf16[64,512]{1,0:T(8,128)(2,1)S(1)} %second.1.refs_0_), channel_id=1, source_target_pairs={{0,2},{1,3},{2,0},{3,1},{4,6},{5,7},{6,4},{7,5},{8,10},{9,11},{10,... | collective-permute-start | bytes 196616 | tf_op jit(solution)/shard_map/ppermute | solution.py:170
  21.4 3.8 %collective-permute-start.3 = (bf16[64,512]{1,0:T(8,128)(2,1)S(1)}, bf16[64,512]{1,0:T(8,128)(2,1)S(1)}, u32[]{:S(2)}, u32[]{:S(2)}) collective-permute-start(bf16[64,512]{1,0:T(8,128)(2,1)S(1)} %second.1.refs_0_), channel_id=1, source_target_pairs={{0,1},{1,0},{2,3},{3,2},{4,5},{5,4},{6,7},{7,6},{8,9},{9,8},{10,11... | collective-permute-start | bytes 196616 | tf_op jit(solution)/shard_map/ppermute | solution.py:170
  25.2 1.3 %collective-permute-start.2 = (bf16[64,512]{1,0:T(8,128)(2,1)S(1)}, bf16[64,512]{1,0:T(8,128)(2,1)S(1)}, u32[]{:S(2)}, u32[]{:S(2)}) collective-permute-start(bf16[64,512]{1,0:T(8,128)(2,1)S(1)} %collective-permute-done.1.refs_0_), channel_id=1, source_target_pairs={{0,1},{1,0},{2,3},{3,2},{4,5},{5,4},{6,7},{7,6},{8,9},{9,8},{10,11... | collective-permute-start | bytes 196616 | tf_op jit(solution)/shard_map/ppermute | solution.py:170
  25.7 4.3 %copy-start.3 = (s32[4,6]{1,0:T(4,128)S(1)}, s32[4,6]{1,0:T(4,128)}, u32[]{:S(2)}) copy-start(s32[4,6]{1,0:T(4,128)} %ids_hbm.1) | copy-start | bytes 292
  27.4 10.6 %all-to-all-start.1 = ((bf16[32,2,896]{2,1,0:T(2,128)(2,1)}), bf16[32,2,896]{2,1,0:T(2,128)(2,1)S(1)}, u32[]{:S(2)}, u32[]{:S(2)}) async-start(bf16[32,2,896]{2,1,0:T(2,128)(2,1)} %shard_map.66), calls=%async_computation.1 | async-start | bytes 229376 | tf_op jit(solution)/shard_map/all_to_all | solution.py:225

commit v4 on v3

--- a/solution.py
+++ b/solution.py
@@ -53,7 +53,7 @@
     pick_ref[...] = jnp.concatenate(pick, axis=0).astype(jnp.bfloat16)
 
 
-def dispatch_kernel(nodes, lanes_local, slots, tok_hbm, ids_hbm, codes_hbm, out_ref, tok_ref, ids_ref, codes_ref, sems):
+def dispatch_kernel(nodes, lanes_local, slots, tok_hbm, ids_hbm, codes_hbm, out_ref, named_ref, tok_ref, ids_ref, codes_ref, sems):
     copies = [
         pltpu.make_async_copy(source, target, sems.at[i])
         for i, (source, target) in enumerate(((ids_hbm, ids_ref), (codes_hbm, codes_ref), (tok_hbm, tok_ref)))
@@ -61,6 +61,7 @@
     for copy in copies:
         copy.start()
     copies[0].wait()
+    named_ref[...] = ids_ref[...]
     rows, top = ids_ref.shape
     half = tok_ref.shape[1] // 2
     ids = ids_ref[...].astype(jnp.float32)
@@ -149,11 +150,14 @@
     half = width // 2
     rows = devices * slots
     per_lane, out_width = gate_proj.shape[1], down_proj.shape[1]
-    send = pl.pallas_call(
+    send, named = pl.pallas_call(
         functools.partial(dispatch_kernel, nodes, locals_, slots),
-        out_shape=jax.ShapeDtypeStruct((devices, slots, half + LANES), jnp.bfloat16),
+        out_shape=(
+            jax.ShapeDtypeStruct((devices, slots, half + LANES), jnp.bfloat16),
+            jax.ShapeDtypeStruct(expert_ids.shape, expert_ids.dtype),
+        ),
         in_specs=[HBM] * 3,
-        out_specs=VMEM,
+        out_specs=(VMEM, VMEM),
         scratch_shapes=[
             pltpu.VMEM(tokens.shape, tokens.dtype),
             pltpu.VMEM(expert_ids.shape, expert_ids.dtype),
@@ -161,9 +165,18 @@
             pltpu.SemaphoreType.DMA((3,)),
         ],
         compiler_params=small(4096),
-        cost_estimate=pl.CostEstimate(flops=10**10, bytes_accessed=40 << 20, transcendentals=0),
         name="dispatch",
     )(*hbm(tokens, expert_ids, gate_codes))
+    pick = pl.pallas_call(
+        functools.partial(pick_kernel, nodes, locals_, slots),
+        out_shape=jax.ShapeDtypeStruct((locals_ * own_rows, rows), jnp.bfloat16),
+        in_specs=[VMEM],
+        out_specs=VMEM,
+        compiler_params=small(4096),
+        cost_estimate=pl.CostEstimate(flops=10**10, bytes_accessed=40 << 20, transcendentals=0),
+        name="pick",
+    )(named)
+    send, pick = lax.optimization_barrier((send, pick))
     arrived = lax.all_to_all(send, EVERY, split_axis=0, concat_axis=0, tiled=True)
 
     def flip(array, bit):
@@ -211,15 +224,7 @@
             far[key ^ (1 << b)] = flip(piece, 1 << b)
     del far[0]
     near = down({0: hidden, 1: flip(hidden, 1)})
-    relayed = {key ^ 1: flip(piece, 1) for key, piece in far.items()}
-    pick = pl.pallas_call(
-        functools.partial(pick_kernel, nodes, locals_, slots),
-        out_shape=jax.ShapeDtypeStruct((locals_ * own_rows, rows), jnp.bfloat16),
-        in_specs=[VMEM],
-        out_specs=VMEM,
-        compiler_params=small(4096),
-        name="pick",
-    )(expert_ids)
+    relayed = {key ^ 1: flip(hidden, key ^ 1) for key in far}
     lean = down(far, near)
     contrib = down(relayed, lean, jax.ShapeDtypeStruct((devices, slots, out_width), jnp.bfloat16))
     back = lax.all_to_all(contrib, EVERY, split_axis=0, concat_axis=0, tiled=True)

time: 39 us -> 37.9 us (0.972)
  blocking collectives: 17.4 us -> 27.7 us
  waiting for transfers between devices: 12.9 us -> 3.54 us
  starting transfers between devices: 3.16 us -> 1.93 us
  Pallas kernels: 5.25 us -> 4.44 us
    all_to_all x0 -> x1, blocking collectives: none -> 10.3 us  [layer(): lax.all_to_all(contrib, EVERY, split_axis=0, concat_axis=0, tiled=True)]
    all_to_all x1 -> x0, waiting for transfers between devices: 7.89 us -> none  [layer(): lax.all_to_all(contrib, EVERY, split_axis=0, concat_axis=0, tiled=True)]
    all_to_all x1 -> x0, starting transfers between devices: 2.57 us -> none  [layer(): lax.all_to_all(contrib, EVERY, split_axis=0, concat_axis=0, tiled=True)]
    ppermute x4, waiting for transfers between devices: 4.97 us -> 3.54 us  [flip(): return lax.ppermute(array, 'local', [(i, i ^ bit) for i in range(locals_)])]
    ppermute x4, starting transfers between devices: 0.59 us -> 1.93 us  [flip(): return lax.ppermute(array, 'local', [(i, i ^ bit) for i in range(locals_)])]
    pallas_call x3, Pallas kernels: 1.68 us -> 1.03 us  [down(): pl.pallas_call(functools.partial(down_kernel, tuple(pieces), near is not...]
  transfers between devices with their start and end apart: 5 -> 4, of which waited for: 4 -> 2; matrix products, arithmetic and copies ran while one was open for 0% -> 0% of each run, Pallas kernels for 4% -> 4%
where the time goes in v4:
time: 37.9 us; the launch traced here: 37.7 us
  blocking collectives  27.7 us (73%)
  Pallas kernels  4.44 us (12%)
  waiting for transfers between devices  3.54 us (9%)
  starting transfers between devices  1.93 us (5%)
    all_to_all x1, blocking collectives, layer(): lax.all_to_all(send, EVERY, split_axis=0, concat_axis=0, tiled=True)  17.4 us
    all_to_all x1, blocking collectives, layer(): lax.all_to_all(contrib, EVERY, split_axis=0, concat_axis=0, tiled=True)  10.3 us
    ppermute x4, waiting for transfers between devices, flip(): return lax.ppermute(array, 'local', [(i, i ^ bit) for i in range(locals_)])  3.54 us
    ppermute x4, starting transfers between devices, flip(): return lax.ppermute(array, 'local', [(i, i ^ bit) for i in range(locals_)])  1.93 us
    pallas_call x1, Pallas kernels, layer(): pl.pallas_call(functools.partial(dispatch_kernel, nodes, locals_, slots),...  1.16 us
    pallas_call x3, Pallas kernels, down(): pl.pallas_call(functools.partial(down_kernel, tuple(pieces), near is not...  1.03 us
    pallas_call x1, Pallas kernels, layer(): pl.pallas_call(functools.partial(first_kernel, half, top), out_shape=(jax...  0.76 us
  transfers between devices with their start and end apart: 4, of which 2 were waited for; matrix products, arithmetic and copies ran while one was open for 0% of the time, Pallas kernels for 4%

profile of v4, /device:TPU:0, one launch (start us, length us, event | category | flops | bytes accessed | tf_op | source)
XLA Modules:
  0.0 37.7 jit_solution(8781602392487923521)
XLA Ops:
  0.0 1.2 %dispatch.1 = (bf16[32,2,1920]{2,1,0:T(2,128)(2,1)S(1)}, s32[4,6]{1,0:T(4,128)S(1)}) custom-call(bf16[4,3584]{1,0:T(4,128)(2,1)} %tok_hbm.1, s32[4,6]{1,0:T(4,128)} %ids_hbm.1, s32[4,6]{1,0:T(4,128)} %codes_hbm.1), custom_call_target="tpu_custom_call" | custom-call | tf_op jit(solution)/shard_map/dispatch/pallas_call | solution.py:153
  1.2 0.0 copy-start.1
  1.2 0.0 copy-start.2
  1.2 0.1 pick.1.pick_ref
  1.3 17.4 %all_to_all.10.mine_ref = bf16[32,2,1920]{2,1,0:T(2,128)(2,1)S(1)} all-to-all(bf16[32,2,1920]{2,1,0:T(2,128)(2,1)S(1)} %get-tuple-element.14), channel_id=1, replica_groups=mesh['node'=8,'local'=4] {'node','local'}, dimensions={0} | all-to-all | bytes 491520 | tf_op jit(solution)/shard_map/all_to_all | solution.py:180
  18.7 0.0 collective-permute-start
  18.7 0.0 copy-done.1
  18.7 0.0 copy-done.2
  18.7 0.8 %first.1 = (f32[64,1024]{1,0:T(8,128)S(1)}, f32[64,128]{1,0:T(8,128)S(1)}) custom-call(bf16[32,2,1920]{2,1,0:T(2,128)(2,1)S(1)} %all_to_all.10.mine_ref, bf16[3584,512]{1,0:T(8,128)(2,1)S(1)} %copy-done.1, bf16[3584,512]{1,0:T(8,128)(2,1)S(1)} %copy-done.2), custom_call_target="tpu_custom_call" | custom-call | tf_op jit(solution)/shard_map/first/pallas_call | solution.py:186
  19.4 0.7 %collective-permute-done.other_ref = bf16[32,2,1920]{2,1,0:T(2,128)(2,1)S(1)} collective-permute-done((bf16[32,2,1920]{2,1,0:T(2,128)(2,1)S(1)}, bf16[32,2,1920]{2,1,0:T(2,128)(2,1)S(1)}, u32[]{:S(2)}, u32[]{:S(2)}) %collective-permute-start) | collective-permute-done | bytes 245792 | tf_op jit(solution)/shard_map/ppermute | solution.py:183
  20.2 0.0 copy-start
  20.2 0.7 %second.1.refs_0_ = bf16[64,512]{1,0:T(8,128)(2,1)S(1)} custom-call(f32[64,1024]{1,0:T(8,128)S(1)} %get-tuple-element.15.sum_ref, f32[64,128]{1,0:T(8,128)S(1)} %get-tuple-element.16.scale_ref, bf16[32,2,1920]{2,1,0:T(2,128)(2,1)S(1)} %collective-permute-done.other_ref, bf16[3584,512]{1,0:T(8,128)(2,1)S(1)} %copy-done.1, bf16[3584,512]{1,0:T(8,128)(2,1)S(1)} %copy-done.2), custom_call_target="tpu_custom_call" | custom-call | tf_op jit(solution)/shard_map/second/pallas_call | solution.py:197
  20.8 0.2 collective-permute-start.3
  21.0 0.7 %collective-permute-start.2 = (bf16[64,512]{1,0:T(8,128)(2,1)S(1)}, bf16[64,512]{1,0:T(8,128)(2,1)S(1)}, u32[]{:S(2)}, u32[]{:S(2)}) collective-permute-start(bf16[64,512]{1,0:T(8,128)(2,1)S(1)} %second.1.refs_0_), channel_id=1, source_target_pairs={{0,2},{1,3},{2,0},{3,1},{4,6},{5,7},{6,4},{7,5},{8,10},{9,11},{10,... | collective-permute-start | bytes 196616 | tf_op jit(solution)/shard_map/ppermute | solution.py:183
  21.7 1.1 %collective-permute-start.1 = (bf16[64,512]{1,0:T(8,128)(2,1)S(1)}, bf16[64,512]{1,0:T(8,128)(2,1)S(1)}, u32[]{:S(2)}, u32[]{:S(2)}) collective-permute-start(bf16[64,512]{1,0:T(8,128)(2,1)S(1)} %second.1.refs_0_), channel_id=1, source_target_pairs={{0,3},{1,2},{2,1},{3,0},{4,7},{5,6},{6,5},{7,4},{8,11},{9,10},{10,... | collective-permute-start | bytes 196616 | tf_op jit(solution)/shard_map/ppermute | solution.py:183
  22.8 0.0 collective-permute-done.3.refs_1_
  22.8 0.0 copy-done
  22.8 0.4 %shard_map.64.refs_2_ = f32[64,896]{1,0:T(8,128)S(1)} custom-call(bf16[64,512]{1,0:T(8,128)(2,1)S(1)} %second.1.refs_0_, bf16[64,512]{1,0:T(8,128)(2,1)S(1)} %collective-permute-done.3.refs_1_, bf16[2048,896]{1,0:T(8,128)(2,1)S(1)} %copy-done), custom_call_target="tpu_custom_call" | custom-call | flops 117440512 | bytes 1835008 | tf_op jit(solution)/shard_map/pallas_call | solution.py:208
  23.2 2.8 %collective-permute-done.2.refs_0_ = bf16[64,512]{1,0:T(8,128)(2,1)S(1)} collective-permute-done((bf16[64,512]{1,0:T(8,128)(2,1)S(1)}, bf16[64,512]{1,0:T(8,128)(2,1)S(1)}, u32[]{:S(2)}, u32[]{:S(2)}) %collective-permute-start.2) | collective-permute-done | bytes 65568 | tf_op jit(solution)/shard_map/ppermute | solution.py:183
  26.0 0.3 shard_map.65.refs_2_
  26.3 0.0 collective-permute-done.1.refs_0_
  26.3 0.3 shard_map.66
  26.6 10.3 %all_to_all.11.back_ref = bf16[32,2,896]{2,1,0:T(2,128)(2,1)S(1)} all-to-all(bf16[32,2,896]{2,1,0:T(2,128)(2,1)S(1)} %shard_map.66), channel_id=1, replica_groups=mesh['node'=8,'local'=4] {'node','local'}, dimensions={0} | all-to-all | bytes 229376 | tf_op jit(solution)/shard_map/all_to_all | solution.py:230
  37.0 0.8 %combine.1 = bf16[4,3584]{1,0:T(4,128)(2,1)} custom-call(bf16[16,64]{1,0:T(8,128)(2,1)S(1)} %pick.1.pick_ref, bf16[32,2,896]{2,1,0:T(2,128)(2,1)S(1)} %all_to_all.11.back_ref), custom_call_target="tpu_custom_call" | custom-call | tf_op jit(solution)/shard_map/combine/pallas_call | solution.py:231
Async XLA Ops:
  1.2 17.5 %copy-start.1 = (bf16[3584,512]{1,0:T(8,128)(2,1)S(1)}, bf16[3584,512]{1,0:T(8,128)(2,1)}, u32[]{:S(2)}) copy-start(bf16[3584,512]{1,0:T(8,128)(2,1)} %gate_ref.3) | copy-start | bytes 11010052
  1.2 17.5 %copy-start.2 = (bf16[3584,512]{1,0:T(8,128)(2,1)S(1)}, bf16[3584,512]{1,0:T(8,128)(2,1)}, u32[]{:S(2)}) copy-start(bf16[3584,512]{1,0:T(8,128)(2,1)} %up_ref.3) | copy-start | bytes 11010052
  18.7 1.5 %collective-permute-start = (bf16[32,2,1920]{2,1,0:T(2,128)(2,1)S(1)}, bf16[32,2,1920]{2,1,0:T(2,128)(2,1)S(1)}, u32[]{:S(2)}, u32[]{:S(2)}) collective-permute-start(bf16[32,2,1920]{2,1,0:T(2,128)(2,1)S(1)} %all_to_all.10.mine_ref), channel_id=1, source_target_pairs={{0,1},{1,0},{2,3},{3,2},{4,5},{5,4},{6,7},{7,6},{8,9},{9,8},{10,11... | collective-permute-start | bytes 737288 | tf_op jit(solution)/shard_map/ppermute | solution.py:183
  20.2 2.6 %copy-start = (bf16[2048,896]{1,0:T(8,128)(2,1)S(1)}, bf16[2048,896]{1,0:T(8,128)(2,1)}, u32[]{:S(2)}) copy-start(bf16[2048,896]{1,0:T(8,128)(2,1)} %refs_1_.3) | copy-start | bytes 11010052
  20.8 1.9 %collective-permute-start.3 = (bf16[64,512]{1,0:T(8,128)(2,1)S(1)}, bf16[64,512]{1,0:T(8,128)(2,1)S(1)}, u32[]{:S(2)}, u32[]{:S(2)}) collective-permute-start(bf16[64,512]{1,0:T(8,128)(2,1)S(1)} %second.1.refs_0_), channel_id=1, source_target_pairs={{0,1},{1,0},{2,3},{3,2},{4,5},{5,4},{6,7},{7,6},{8,9},{9,8},{10,11... | collective-permute-start | bytes 196616 | tf_op jit(solution)/shard_map/ppermute | solution.py:183
  21.0 5.0 %collective-permute-start.2 = (bf16[64,512]{1,0:T(8,128)(2,1)S(1)}, bf16[64,512]{1,0:T(8,128)(2,1)S(1)}, u32[]{:S(2)}, u32[]{:S(2)}) collective-permute-start(bf16[64,512]{1,0:T(8,128)(2,1)S(1)} %second.1.refs_0_), channel_id=1, source_target_pairs={{0,2},{1,3},{2,0},{3,1},{4,6},{5,7},{6,4},{7,5},{8,10},{9,11},{10,... | collective-permute-start | bytes 196616 | tf_op jit(solution)/shard_map/ppermute | solution.py:183
  21.7 4.6 %collective-permute-start.1 = (bf16[64,512]{1,0:T(8,128)(2,1)S(1)}, bf16[64,512]{1,0:T(8,128)(2,1)S(1)}, u32[]{:S(2)}, u32[]{:S(2)}) collective-permute-start(bf16[64,512]{1,0:T(8,128)(2,1)S(1)} %second.1.refs_0_), channel_id=1, source_target_pairs={{0,3},{1,2},{2,1},{3,0},{4,7},{5,6},{6,5},{7,4},{8,11},{9,10},{10,... | collective-permute-start | bytes 196616 | tf_op jit(solution)/shard_map/ppermute | solution.py:183
